TPU v7x, 32 devices: a whole 2x2x4 slice. The times are simulated.
32 devices in a mesh: trunk: 4 (over x, core), branch: 8 (over z, y).
Axes of the slice: x: 2, y: 2, z: 4, core: 2. Of those that a mesh axis runs over, the one named last changes fastest.
Arguments:
- queries: bfloat16 [4, 1024, 4096], P('trunk', 'branch'), may hold values from -160 to 160
- keys_values: bfloat16 [4, 1024, 2, 512], P('trunk', 'branch'), may hold values from -7 to 7
- out_grad: bfloat16 [4, 1024, 4096], P('trunk', 'branch'), may hold values from -6 to 6
- trunk_kv: bfloat16 [4, 8, 2, 16, 512], P('trunk', 'branch'), may hold values from -6 to 6
- branch_of: int32 [4, 1024], P('trunk', 'branch'), may hold values from 0 to 15, never falling along the last dimension, each value on 1 to 128 neighbouring positions
- branch_reach: int32 [4, 16], P('trunk'), may hold values from 1 to 4
- ancestors: int32 [4, 8, 4], P('trunk', 'branch'), may hold values from 0 to 7
Outputs:
- attended: bfloat16 [4, 1024, 4096], P('trunk', 'branch')
- query_grad: bfloat16 [4, 1024, 4096], P('trunk', 'branch')
- kv_grad: float32 [4, 1024, 2, 512], P('trunk', 'branch')
- trunk_grad: float32 [4, 8, 2, 16, 512], P('trunk', 'branch')
Inputs may be any that keep to these rules, and one draw needn't show every extreme that they name: `branch_of`: ids never fall along a row; each branch covers 1 to 128 consecutive tokens. `ancestors`: entry d names the branch index of the device at trunk index d that holds the segment read at depth d.
All inputs are finite; a program needn't handle non-finite values.
Results may differ from a plain program's by a relative error of at most 0.005.
Values may be sent and summed in bfloat16 or wider, within the bound.
No kernel may reach another device: no remote copies, remote signals or barrier semaphores. Data moves between devices by JAX's collectives and lax.ppermute only.
A program may use at most 128 MiB of HBM per device.

v0:
```python
import math

import jax
import jax.numpy as jnp
from jax import lax
from jax.sharding import PartitionSpec as P

HQ = 32
KVH = 4
DH = 128


def from_behind(block, axis, distance):
    devices = range(lax.axis_size(axis))
    route = [(i - distance, i) for i in devices if i - distance in devices]
    return lax.ppermute(block, axis, route)


def build_allowed(tags, earlier_tags, reach_rows, seg_len, depth_count):
    trunk_depth = jnp.arange(depth_count * seg_len, dtype=jnp.int32) // seg_len
    trunk_ok = trunk_depth[None, :] < reach_rows[:, None]
    earlier_ok = earlier_tags[None, :] == tags[:, None]
    position = jnp.arange(tags.shape[0], dtype=jnp.int32)
    own_ok = (tags[None, :] == tags[:, None]) & (position[None, :] <= position[:, None])
    return jnp.concatenate([trunk_ok, earlier_ok, own_ok], axis=1)


def attend_block(query_rows, grad_rows, key_rows, value_rows, allowed):
    head_scale = 1.0 / math.sqrt(DH)
    group = HQ // KVH
    n_rows = query_rows.shape[0]
    outputs, query_grads, key_grads, value_grads = ([], [], [], [])
    for head_group in range(KVH):
        query_part = query_rows[:, head_group * group * DH : (head_group + 1) * group * DH].reshape(
            n_rows, group, DH
        )
        grad_part = grad_rows[:, head_group * group * DH : (head_group + 1) * group * DH].reshape(
            n_rows, group, DH
        )
        key_part = key_rows[:, head_group * DH : (head_group + 1) * DH]
        value_part = value_rows[:, head_group * DH : (head_group + 1) * DH]
        scores = (
            jnp.einsum("qrd,kd->rqk", query_part, key_part, preferred_element_type=jnp.float32)
            * head_scale
        )
        masked = jnp.where(allowed[None], scores, -1e30)
        highest = jnp.max(masked, axis=-1, keepdims=True)
        expo = jnp.exp(masked - highest)
        weights = expo / jnp.sum(expo, axis=-1, keepdims=True)
        weights_bf = weights.astype(jnp.bfloat16)
        output = jnp.einsum(
            "rqk,kd->qrd", weights_bf, value_part, preferred_element_type=jnp.float32
        ).reshape(n_rows, group * DH)
        grad_weights = jnp.einsum(
            "qrd,kd->rqk", grad_part, value_part, preferred_element_type=jnp.float32
        )
        row_mean = jnp.sum(weights * grad_weights, axis=-1, keepdims=True)
        score_grad = (weights * (grad_weights - row_mean)).astype(jnp.bfloat16)
        outputs.append(output)
        query_grads.append(
            (
                jnp.einsum("rqk,kd->qrd", score_grad, key_part, preferred_element_type=jnp.float32)
                * head_scale
            ).reshape(n_rows, group * DH)
        )
        key_grads.append(
            jnp.einsum("rqk,qrd->kd", score_grad, query_part, preferred_element_type=jnp.float32)
            * head_scale
        )
        value_grads.append(
            jnp.einsum("rqk,qrd->kd", weights_bf, grad_part, preferred_element_type=jnp.float32)
        )
    attended = jnp.concatenate(outputs, axis=1).astype(jnp.bfloat16)
    query_grad = jnp.concatenate(query_grads, axis=1).astype(jnp.bfloat16)
    return (
        attended,
        query_grad,
        jnp.concatenate(key_grads, axis=1),
        jnp.concatenate(value_grads, axis=1),
    )


def on_device(queries, keys_values, out_grad, trunk_kv, branch_of, branch_reach, ancestors):
    depth_count = lax.axis_size("trunk")
    n_branch = lax.axis_size("branch")
    seg_len = trunk_kv.shape[3]
    width = trunk_kv.shape[4]
    block_len = queries.shape[1]
    trunk_len = depth_count * seg_len
    requested = lax.all_to_all(ancestors[0, 0], "trunk", split_axis=0, concat_axis=0, tiled=True)
    own_segment = trunk_kv[0]
    piece = lax.all_gather(own_segment, "branch", axis=0, tiled=True)
    owner_index = jnp.arange(piece.shape[0], dtype=jnp.int32)
    hits = (requested[:, None] == owner_index[None, :]).astype(jnp.bfloat16)
    chosen = jnp.einsum("tn,nslc->tslc", hits, piece, preferred_element_type=jnp.float32)
    picked = chosen.astype(jnp.bfloat16)
    fetched = lax.all_to_all(picked, "trunk", split_axis=0, concat_axis=0, tiled=True)
    branch_ids = branch_of[0]
    tags = branch_ids + 1
    earlier_kv, earlier_tags = from_behind((keys_values[0], tags), "branch", 1)
    reach_table = branch_reach[0]
    branch_index = jnp.arange(reach_table.shape[0], dtype=jnp.int32)
    reach_rows = jnp.sum(
        jnp.where(branch_ids[:, None] == branch_index[None, :], reach_table[None, :], 0), axis=1
    )
    allowed = build_allowed(tags, earlier_tags, reach_rows, seg_len, depth_count)
    key_rows = jnp.concatenate(
        [fetched[:, 0].reshape(trunk_len, width), earlier_kv[:, 0], keys_values[0, :, 0]], axis=0
    )
    value_rows = jnp.concatenate(
        [fetched[:, 1].reshape(trunk_len, width), earlier_kv[:, 1], keys_values[0, :, 1]], axis=0
    )
    attended, query_grad, key_grad, value_grad = attend_block(
        queries[0], out_grad[0], key_rows, value_rows, allowed
    )
    earlier_part = jnp.stack(
        [
            key_grad[trunk_len : trunk_len + block_len],
            value_grad[trunk_len : trunk_len + block_len],
        ],
        axis=1,
    )
    own_part = jnp.stack(
        [key_grad[trunk_len + block_len :], value_grad[trunk_len + block_len :]], axis=1
    )
    from_next = from_behind(earlier_part.astype(jnp.bfloat16), "branch", -1).astype(
        earlier_part.dtype
    )
    kv_grad = (own_part + from_next)[None]
    trunk_part = jnp.stack(
        [
            key_grad[:trunk_len].reshape(depth_count, seg_len, width),
            value_grad[:trunk_len].reshape(depth_count, seg_len, width),
        ],
        axis=1,
    )
    returned = lax.all_to_all(trunk_part, "trunk", split_axis=0, concat_axis=0, tiled=True)
    owner_index = jnp.arange(n_branch, dtype=jnp.int32)
    owners_hit = (requested[None, :] == owner_index[:, None]).astype(jnp.float32)
    dense = jnp.einsum("ot,tslc->oslc", owners_hit, returned, precision=lax.Precision.HIGHEST)
    mine = lax.psum_scatter(dense, "branch", scatter_dimension=0, tiled=True)
    trunk_grad = mine[None]
    return (attended[None], query_grad[None], kv_grad, trunk_grad)


def solution(mesh):
    return jax.shard_map(
        on_device,
        mesh=mesh,
        in_specs=(
            P("trunk", "branch", None),
            P("trunk", "branch", None, None),
            P("trunk", "branch", None),
            P("trunk", "branch", None, None, None),
            P("trunk", "branch"),
            P("trunk", None),
            P("trunk", "branch", None),
        ),
        out_specs=(
            P("trunk", "branch", None),
            P("trunk", "branch", None),
            P("trunk", "branch", None, None),
            P("trunk", "branch", None, None, None),
        ),
        check_vma=False,
    )
```

profile of v0, /device:TPU:0, one launch (start us, length us, event | category | flops | bytes accessed | tf_op | source)
XLA Modules:
  0.0 184.4 jit_solution(7487720587268420429)
XLA Ops:
  7.2 1.4 copy.141
  8.6 4.2 %all-to-all-start = ((s32[4,1,1]{2,1,0:T(1,128)}), s32[4,1,1]{2,1,0:T(1,128)S(1)}, u32[]{:S(2)}, u32[]{:S(2)}) async-start(s32[4,1,1]{2,1,0:T(1,128)} %copy.141), calls=%async_computation | async-start | bytes 4096 | tf_op jit(solution)/shard_map/all_to_all | solution.py:90
  12.8 0.7 broadcast_add_fusion
  13.5 3.9 %collective-permute-start.1 = (s32[128]{0:T(128)S(1)}, s32[128]{0:T(128)S(1)}, u32[]{:S(2)}, u32[]{:S(2)}) collective-permute-start(s32[128]{0:T(128)S(1)} %broadcast_add_fusion), channel_id=1, source_target_pairs={{0,1},{1,2},{2,3},{3,4},{4,5},{5,6},{6,7},{8,9},{9,10},{10,11},{11... | collective-permute-start | bytes 1544 | tf_op jit(solution)/shard_map/ppermute | solution.py:16
  17.4 1.0 copy.208
  18.3 3.4 %collective-permute-start = (bf16[128,2,512]{2,0,1:T(8,128)(2,1)S(1)}, bf16[128,2,512]{2,0,1:T(8,128)(2,1)S(1)}, u32[]{:S(2)}, u32[]{:S(2)}) collective-permute-start(bf16[128,2,512]{2,0,1:T(8,128)(2,1)S(1)} %bitcast.321), channel_id=1, source_target_pairs={{0,1},{1,2},{2,3},{3,4},{4,5},{5,6},{6,7},{8,9},{9,10},{10,11},{11... | collective-permute-start | bytes 786440 | tf_op jit(solution)/shard_map/ppermute | solution.py:16
  21.8 0.7 add_bitcast_fusion
  22.5 31.9 %all-gather = bf16[8,1,2,16,512]{4,3,2,1,0:T(8,128)(2,1)S(1)} all-gather(bf16[1,1,2,16,512]{4,3,2,1,0:T(8,128)(2,1)} %param.10), channel_id=2, replica_groups=mesh['trunk'=4,'branch'=8] {'branch'}, dimensions={0}, use_global_device_ids=true | all-gather | bytes 294912 | tf_op jit(solution)/shard_map/all_gather | solution.py:92
  54.4 0.7 copy.149
  55.0 0.9 fusion.63
  55.9 0.6 copy-done.2
  56.5 0.7 copy.158
  57.2 0.9 fusion.62
  58.5 0.3 convolution_convert_fusion.4
  58.8 0.7 copy.143
  59.5 3.3 %all-to-all-start.1 = ((bf16[4,2,16,512]{3,2,1,0:T(8,128)(2,1)}), bf16[4,2,16,512]{3,2,1,0:T(8,128)(2,1)S(1)}, u32[]{:S(2)}, u32[]{:S(2)}) async-start(bf16[4,2,16,512]{3,2,1,0:T(8,128)(2,1)} %copy.143), calls=%async_computation.1 | async-start | bytes 262144 | tf_op jit(solution)/shard_map/all_to_all | solution.py:97
  63.0 4.4 %all-to-all-done.1 = bf16[4,2,16,512]{3,2,1,0:T(8,128)(2,1)S(1)} async-done(((bf16[4,2,16,512]{3,2,1,0:T(8,128)(2,1)}), bf16[4,2,16,512]{3,2,1,0:T(8,128)(2,1)S(1)}, u32[]{:S(2)}, u32[]{:S(2)}) %all-to-all-start.1) | async-done | bytes 131104 | tf_op jit(solution)/shard_map/all_to_all | solution.py:97
  67.5 0.6 fusion.65
  68.0 1.5 convolution_bitcast_fusion.4
  69.5 1.5 convolution_convert_fusion
  71.1 0.3 multiply_reduce_fusion
  71.7 0.3 fusion.27
  72.0 0.3 fusion.23
  72.6 0.5 fusion.68
  73.3 1.5 convolution_convert_fusion.3
  74.9 1.5 convolution_bitcast_fusion.7
  76.4 0.3 multiply_reduce_fusion.3
  77.0 0.3 fusion.24
  77.3 1.1 fusion.20
  78.3 0.5 fusion.66
  78.9 0.4 copy-done.17
  79.3 1.5 convolution_convert_fusion.1
  80.9 0.8 convolution_bitcast_fusion.5
  81.7 0.3 multiply_reduce_fusion.1
  82.3 0.3 fusion.26
  82.6 1.0 fusion.22
  83.6 1.6 fusion.67
  85.2 0.8 convolution_bitcast_fusion.6
  86.2 0.7 pad_maximum_fusion.8
  86.9 1.0 pad_maximum_fusion.3
  87.9 2.3 %convolution_convert_fusion.2 = bf16[128,8,128]{2,0,1:T(8,128)(2,1)} fusion(bf16[320,512]{1,0:T(8,128)(2,1)S(1)} %copy-done.18, f32[8,128]{1,0:T(8,128)S(1)} %get-tuple-element.46, bf16[128,8,128]{0,2,1:T(8,128)(2,1)S(1)} %bitcast.328, pred[128,320]{0,1:T(8,128)(4,1)} %copy-done.22, bf16[320,512]{1,0:T(8,128)(2,1)S(1)} %get-tuple-element.59), kind=kOutput, calls=%fused_computation.46 | convolution fusion | flops 169542976 | bytes 733184 | tf_op jit(solution)/shard_map/rqk,kd->qrd/dot_general | solution.py:51
  90.2 1.7 multiply_reduce_fusion.2
  92.1 0.3 fusion.25
  92.5 0.6 pad_maximum_fusion.9
  93.2 1.8 copy.157
  95.0 0.8 copy.166
  95.8 1.8 copy.154
  97.8 1.8 copy.156
  99.6 1.8 copy.165
  101.4 1.8 copy.155
  103.3 0.7 pad_maximum_fusion.7
  104.0 3.4 %all-to-all-start.2 = ((f32[4,2,16,512]{3,2,1,0:T(8,128)}), f32[4,2,16,512]{3,2,1,0:T(8,128)S(1)}, u32[]{:S(2)}, u32[]{:S(2)}) async-start(f32[4,2,16,512]{3,2,1,0:T(8,128)} %pad_maximum_fusion.7), calls=%async_computation.2 | async-start | bytes 524288 | tf_op jit(solution)/shard_map/all_to_all | solution.py:137
  107.5 0.7 pad_maximum_fusion.6
  108.2 1.3 collective-permute-start.2
  109.5 2.2 %pad_maximum_fusion = bf16[1,128,4096]{2,1,0:T(8,128)(2,1)} fusion(bf16[1,128,1024]{2,1,0:T(8,128)(2,1)S(1)} %copy-done.6, bf16[1,128,1024]{2,1,0:T(8,128)(2,1)} %copy.156, bf16[1,128,1024]{2,1,0:T(8,128)(2,1)} %copy.155, bf16[1,128,1024]{2,1,0:T(8,128)(2,1)} %copy.154), kind=kLoop, calls=%fused_computation.61 | loop fusion | flops 4194304 | bytes 2097152 | tf_op jit(solution)/shard_map/concatenate | solution.py:73
  111.7 0.3 fusion.21
  112.2 1.2 all-to-all-done.2
  113.4 0.6 fusion.38
  114.0 1.1 copy.178
  115.1 1.0 pad_maximum_fusion.1
  116.2 2.8 %collective-permute-done.2 = bf16[128,2,512]{2,0,1:T(8,128)(2,1)} collective-permute-done((bf16[128,2,512]{2,0,1:T(8,128)(2,1)}, bf16[128,2,512]{2,0,1:T(8,128)(2,1)}, u32[]{:S(2)}, u32[]{:S(2)}) %collective-permute-start.2) | collective-permute-done | bytes 262176 | tf_op jit(solution)/shard_map/ppermute | solution.py:16
  119.0 1.0 fusion.28
  120.1 1.2 copy.179
  121.3 56.3 %reduce-scatter.2.cloned.1.call-done = f32[1,2,16,512]{3,2,1,0:T(8,128)} async-done(((f32[8,2,16,512]{3,2,1,0:T(8,128)}), f32[1,2,16,512]{3,2,1,0:T(8,128)}) %reduce-scatter.2.cloned.1.call-update) | async-done | bytes 65552 | tf_op jit(solution)/shard_map/reduce_scatter | solution.py:141
  (76 shorter events, 2.5 us)
Async XLA Ops:
  7.2 47.2 %copy-start.1 = (bf16[1,128,4096]{2,1,0:T(8,128)(2,1)S(1)}, bf16[1,128,4096]{2,1,0:T(8,128)(2,1)}, u32[]{:S(2)}) copy-start(bf16[1,128,4096]{2,1,0:T(8,128)(2,1)} %param.7) | copy-start | bytes 3145732
  8.6 49.7 %all-to-all-start = ((s32[4,1,1]{2,1,0:T(1,128)}), s32[4,1,1]{2,1,0:T(1,128)S(1)}, u32[]{:S(2)}, u32[]{:S(2)}) async-start(s32[4,1,1]{2,1,0:T(1,128)} %copy.141), calls=%async_computation | async-start | bytes 4096 | tf_op jit(solution)/shard_map/all_to_all | solution.py:90
  13.5 49.3 %collective-permute-start.1 = (s32[128]{0:T(128)S(1)}, s32[128]{0:T(128)S(1)}, u32[]{:S(2)}, u32[]{:S(2)}) collective-permute-start(s32[128]{0:T(128)S(1)} %broadcast_add_fusion), channel_id=1, source_target_pairs={{0,1},{1,2},{2,3},{3,4},{4,5},{5,6},{6,7},{8,9},{9,10},{10,11},{11... | collective-permute-start | bytes 1544 | tf_op jit(solution)/shard_map/ppermute | solution.py:16
  18.3 49.0 %collective-permute-start = (bf16[128,2,512]{2,0,1:T(8,128)(2,1)S(1)}, bf16[128,2,512]{2,0,1:T(8,128)(2,1)S(1)}, u32[]{:S(2)}, u32[]{:S(2)}) collective-permute-start(bf16[128,2,512]{2,0,1:T(8,128)(2,1)S(1)} %bitcast.321), channel_id=1, source_target_pairs={{0,1},{1,2},{2,3},{3,4},{4,5},{5,6},{6,7},{8,9},{9,10},{10,11},{11... | collective-permute-start | bytes 786440 | tf_op jit(solution)/shard_map/ppermute | solution.py:16
  55.0 1.5 copy-start.2
  57.2 0.9 copy-start.24
  57.2 0.9 copy-start.25
  59.5 7.9 %all-to-all-start.1 = ((bf16[4,2,16,512]{3,2,1,0:T(8,128)(2,1)}), bf16[4,2,16,512]{3,2,1,0:T(8,128)(2,1)S(1)}, u32[]{:S(2)}, u32[]{:S(2)}) async-start(bf16[4,2,16,512]{3,2,1,0:T(8,128)(2,1)} %copy.143), calls=%async_computation.1 | async-start | bytes 262144 | tf_op jit(solution)/shard_map/all_to_all | solution.py:97
  62.9 6.6 %copy-start.22 = (pred[128,320]{0,1:T(8,128)(4,1)}, pred[128,320]{0,1:T(8,128)(4,1)S(1)}, u32[]{:S(2)}) copy-start(pred[128,320]{0,1:T(8,128)(4,1)S(1)} %pad_add_fusion) | copy-start | bytes 122884
  67.5 3.6 %copy-start.15 = (bf16[320,512]{1,0:T(8,128)(2,1)}, bf16[320,512]{1,0:T(8,128)(2,1)S(1)}, u32[]{:S(2)}) copy-start(bf16[320,512]{1,0:T(8,128)(2,1)S(1)} %get-tuple-element.58) | copy-start | bytes 983044
  71.6 1.0 copy-start.9
  71.7 0.9 copy-start.23
  72.3 1.0 copy-start.16
  73.3 1.6 copy-start.21
  76.9 1.4 copy-start.8
  78.3 1.0 copy-start.17
  79.3 1.5 copy-start.20
  81.7 4.4 %copy-start.12 = (f32[320,128]{1,0:T(8,128)}, f32[320,128]{1,0:T(8,128)S(1)}, u32[]{:S(2)}) copy-start(f32[320,128]{1,0:T(8,128)S(1)} %convolution_bitcast_fusion.5) | copy-start | bytes 491524
  82.3 1.4 copy-start.7
  83.6 1.6 copy-start.19
  85.2 0.9 copy-start.10
  85.2 1.0 copy-start.11
  86.2 1.6 copy-start.18
  90.2 1.8 copy-start
  93.1 4.5 %copy-start.3 = (bf16[128,8,128]{2,0,1:T(8,128)(2,1)S(1)}, bf16[128,8,128]{2,0,1:T(8,128)(2,1)}, u32[]{:S(2)}) copy-start(bf16[128,8,128]{2,0,1:T(8,128)(2,1)} %fusion.20) | copy-start | bytes 786436
  97.6 5.6 %copy-start.13 = (f32[64,512]{1,0:T(8,128)S(1)}, f32[64,512]{1,0:T(8,128)}, u32[]{:S(2)}) copy-start(f32[64,512]{1,0:T(8,128)} %pad_maximum_fusion.8) | copy-start | bytes 393220
  97.6 5.6 %copy-start.14 = (f32[64,512]{1,0:T(8,128)S(1)}, f32[64,512]{1,0:T(8,128)}, u32[]{:S(2)}) copy-start(f32[64,512]{1,0:T(8,128)} %pad_maximum_fusion.9) | copy-start | bytes 393220
  101.4 8.1 %copy-start.6 = (bf16[1,128,1024]{2,1,0:T(8,128)(2,1)S(1)}, bf16[1,128,1024]{2,1,0:T(8,128)(2,1)}, u32[]{:S(2)}) copy-start(bf16[1,128,1024]{2,1,0:T(8,128)(2,1)} %copy.157) | copy-start | bytes 786436
  104.0 9.4 %all-to-all-start.2 = ((f32[4,2,16,512]{3,2,1,0:T(8,128)}), f32[4,2,16,512]{3,2,1,0:T(8,128)S(1)}, u32[]{:S(2)}, u32[]{:S(2)}) async-start(f32[4,2,16,512]{3,2,1,0:T(8,128)} %pad_maximum_fusion.7), calls=%async_computation.2 | async-start | bytes 524288 | tf_op jit(solution)/shard_map/all_to_all | solution.py:137
  107.4 70.2 %reduce-scatter.2.cloned.1.call-start = ((), (), s32[]{:S(2)}) async-start(), calls=%async_computation.4 | async-start | bytes 589824 | tf_op jit(solution)/shard_map/reduce_scatter | solution.py:141
  108.2 10.8 %collective-permute-start.2 = (bf16[128,2,512]{2,0,1:T(8,128)(2,1)}, bf16[128,2,512]{2,0,1:T(8,128)(2,1)}, u32[]{:S(2)}, u32[]{:S(2)}) collective-permute-start(bf16[128,2,512]{2,0,1:T(8,128)(2,1)} %pad_maximum_fusion.6), channel_id=1, source_target_pairs={{1,0},{2,1},{3,2},{4,3},{5,4},{6,5},{7,6},{9,8},{10,9},{11,10},{12... | collective-permute-start | bytes 786440 | tf_op jit(solution)/shard_map/ppermute | solution.py:16
  112.1 3.0 %copy-start.4 = (bf16[1,128,1024]{2,1,0:T(8,128)(2,1)S(1)}, bf16[1,128,1024]{2,1,0:T(8,128)(2,1)}, u32[]{:S(2)}) copy-start(bf16[1,128,1024]{2,1,0:T(8,128)(2,1)} %copy.166) | copy-start | bytes 786436
  112.1 3.0 %copy-start.5 = (bf16[1,128,1024]{2,1,0:T(8,128)(2,1)S(1)}, bf16[1,128,1024]{2,1,0:T(8,128)(2,1)}, u32[]{:S(2)}) copy-start(bf16[1,128,1024]{2,1,0:T(8,128)(2,1)} %copy.165) | copy-start | bytes 786436
Sparse Core Ops, SparseCore 0:
  115.2 62.3 reduce-scatter.1
where the time goes:
time: 185 us; the launch traced here: 184 us
  waiting for transfers between devices  64.8 us (35%)
  blocking collectives  31.9 us (17%)
  matrix products  22.5 us (12%)
  local copies, waits for them, and re-layouts  20.5 us (11%)
  starting transfers between devices  19.6 us (11%)
  between operations  14.5 us (8%)
  other arithmetic  10.6 us (6%)
    reduce_scatter x1, waiting for transfers between devices, on_device(): mine = lax.psum_scatter(dense, 'branch', scatter_dimension=0, tiled=True)  56.3 us
    all_gather x1, blocking collectives, on_device(): piece = lax.all_gather(own_segment, 'branch', axis=0, tiled=True)  31.9 us
    ppermute x3, starting transfers between devices, from_behind(): return lax.ppermute(block, axis, route)  8.61 us
    concatenate x4, local copies, waits for them, and re-layouts, attend_block(): attended = jnp.concatenate(outputs, axis=1).astype(jnp.bfloat16)  7.27 us
    dot_general x4, matrix products, attend_block(): jnp.einsum('rqk,kd->qrd', weights_bf, value_part, preferred_element_type=...  6.93 us
    unnamed x56, local copies, waits for them, and re-layouts  5.21 us
    dot_general x4, matrix products, attend_block(): jnp.einsum('rqk,qrd->kd', weights_bf, grad_part, preferred_element_type=j...  4.66 us
    all_to_all x1, waiting for transfers between devices, on_device(): lax.all_to_all(picked, 'trunk', split_axis=0, concat_axis=0, tiled=True)  4.42 us
  transfers between devices with their start and end apart: 7, of which 4 were waited for; matrix products, arithmetic and copies ran while one was open for 8% of the time, Pallas kernels for 0%

commit v1 on v0

v1 whole, which is shorter than its diff:
```python
import functools
import math

import jax
import jax.numpy as jnp
from jax import lax
from jax.experimental import pallas as pl
from jax.experimental.pallas import tpu as pltpu
from jax.sharding import PartitionSpec as P

HQ = 32
KVH = 4
DH = 128
GROUP = HQ // KVH
BF = jnp.bfloat16
F32 = jnp.float32


def shift(block, axis, distance):
    devices = range(lax.axis_size(axis))
    route = [(i - distance, i) for i in devices if i - distance in devices]
    return lax.ppermute(block, axis, route)


def dot(a, b, ca, cb):
    return lax.dot_general(a, b, (((ca,), (cb,)), ((), ())), preferred_element_type=F32)


def build_allowed(reach_ref, tags_ref, n, trunk_len, seg_len):
    tag_row = tags_ref[0:1, :]
    earlier_row = tags_ref[1:2, :]
    reach_row = jnp.zeros((1, n), jnp.int32)
    for b in range(reach_ref.shape[0]):
        reach_row = jnp.where(tag_row == b + 1, reach_ref[b], reach_row)
    tag_cols = jnp.broadcast_to(tag_row, (n, n))
    key_tags = tag_cols.T
    earlier_tags = jnp.broadcast_to(earlier_row, (n, n)).T
    k_idx = lax.broadcasted_iota(jnp.int32, (n, n), 0)
    q_idx = lax.broadcasted_iota(jnp.int32, (n, n), 1)
    depth = lax.broadcasted_iota(jnp.int32, (trunk_len, n), 0) // seg_len
    trunk_ok = depth < jnp.broadcast_to(reach_row, (trunk_len, n))
    earlier_ok = earlier_tags == tag_cols
    own_ok = (key_tags == tag_cols) & (k_idx <= q_idx)
    as_float = [jnp.where(ok, 0.0, -1e30).astype(F32) for ok in (trunk_ok, earlier_ok, own_ok)]
    return jnp.concatenate(as_float, axis=0)


def attend_kernel(
    reach_ref, tags_ref, q_ref, g_ref, trunk_ref, ek_ref, ev_ref, ok_ref, ov_ref,
    out_ref, dq_ref, dtrunk_ref, dearlier_ref, down_ref, bias_ref,
):
    n = q_ref.shape[0]
    depths, _, seg_len, _ = trunk_ref.shape
    trunk_len = depths * seg_len
    scale = 1.0 / math.sqrt(DH)

    @pl.when(pl.program_id(0) == 0)
    def _():
        bias_ref[...] = build_allowed(reach_ref, tags_ref, n, trunk_len, seg_len)

    keys = jnp.concatenate(
        [trunk_ref[:, 0].reshape(trunk_len, DH), ek_ref[...], ok_ref[...]], axis=0
    )
    values = jnp.concatenate(
        [trunk_ref[:, 1].reshape(trunk_len, DH), ev_ref[...], ov_ref[...]], axis=0
    )
    q_rows = jnp.concatenate([q_ref[:, r * DH : (r + 1) * DH] for r in range(GROUP)], axis=0)
    g_rows = jnp.concatenate([g_ref[:, r * DH : (r + 1) * DH] for r in range(GROUP)], axis=0)
    bias = jnp.concatenate([bias_ref[...]] * GROUP, axis=1)
    scores = dot(keys, q_rows, 1, 1) * scale + bias
    grad_w = dot(values, g_rows, 1, 1)
    highest = jnp.max(scores, axis=0, keepdims=True)
    expo = jnp.exp(scores - highest)
    weights = expo * (1.0 / jnp.sum(expo, axis=0, keepdims=True))
    weights_bf = weights.astype(BF)
    row_mean = jnp.sum(weights * grad_w, axis=0, keepdims=True)
    score_grad = (weights * (grad_w - row_mean)).astype(BF)
    out_t = dot(values, weights_bf, 0, 0)
    dq_t = dot(keys, score_grad, 0, 0) * scale
    for r in range(GROUP):
        cols = slice(r * n, (r + 1) * n)
        out_ref[:, r * DH : (r + 1) * DH] = out_t[:, cols].T.astype(BF)
        dq_ref[:, r * DH : (r + 1) * DH] = dq_t[:, cols].T.astype(BF)
    for which, grad in enumerate(
        (dot(score_grad, q_rows, 1, 0) * scale, dot(weights_bf, g_rows, 1, 0))
    ):
        dtrunk_ref[:, which] = grad[:trunk_len].reshape(depths, seg_len, DH).astype(BF)
        dearlier_ref[which] = grad[trunk_len : trunk_len + n].astype(BF)
        down_ref[which] = grad[trunk_len + n :]


def attend(reach, tags, q, g, trunk, earlier, own):
    n, width = q.shape
    depths, _, seg_len, kv_width = trunk.shape
    heads = kv_width // DH
    part = width // heads
    wide = pl.BlockSpec((n, part), lambda h: (0, h))
    kspec = pl.BlockSpec((n, DH), lambda h: (0, h))
    vspec = pl.BlockSpec((n, DH), lambda h: (0, h + heads))
    tspec = pl.BlockSpec((depths, 2, seg_len, DH), lambda h: (0, 0, 0, h))
    kvspec = pl.BlockSpec((2, n, DH), lambda h: (0, 0, h))
    return pl.pallas_call(
        attend_kernel,
        grid=(heads,),
        in_specs=[
            pl.BlockSpec(memory_space=pltpu.SMEM),
            pl.BlockSpec((2, n), lambda h: (0, 0)),
            wide, wide, tspec, kspec, vspec, kspec, vspec,
        ],
        out_specs=[wide, wide, tspec, kvspec, kvspec],
        out_shape=[
            jax.ShapeDtypeStruct((n, width), BF),
            jax.ShapeDtypeStruct((n, width), BF),
            jax.ShapeDtypeStruct(trunk.shape, BF),
            jax.ShapeDtypeStruct((2, n, kv_width), BF),
            jax.ShapeDtypeStruct((2, n, kv_width), F32),
        ],
        scratch_shapes=[pltpu.VMEM((depths * seg_len + 2 * n, n), F32)],
        name="attend",
    )(reach, tags, q, g, trunk, earlier, earlier, own, own)


def on_device(queries, keys_values, out_grad, trunk_kv, branch_of, branch_reach, ancestors):
    depth_count = lax.axis_size("trunk")
    n_branch = lax.axis_size("branch")
    block_len = queries.shape[1]
    requested = lax.all_to_all(ancestors[0, 0], "trunk", split_axis=0, concat_axis=0, tiled=True)
    own_segment = trunk_kv[0]
    copies = jnp.broadcast_to(own_segment, (n_branch,) + own_segment.shape[1:])
    piece = lax.all_to_all(copies, "branch", split_axis=0, concat_axis=0, tiled=True)
    owner_index = jnp.arange(n_branch, dtype=jnp.int32)
    hits = (requested[:, None] == owner_index[None, :]).astype(BF)
    picked = jnp.einsum("tn,nslc->tslc", hits, piece, preferred_element_type=F32).astype(BF)
    fetched = lax.all_to_all(picked, "trunk", split_axis=0, concat_axis=0, tiled=True)
    tags = branch_of[0] + 1
    own_kv = keys_values[0].reshape(block_len, -1)
    earlier_kv, earlier_tags = shift((own_kv, tags), "branch", 1)
    attended, query_grad, trunk_part, earlier_part, own_part = attend(
        branch_reach[0], jnp.stack([tags, earlier_tags]), queries[0], out_grad[0],
        fetched, earlier_kv, own_kv,
    )
    from_next = shift(earlier_part, "branch", -1)
    returned = lax.all_to_all(trunk_part, "trunk", split_axis=0, concat_axis=0, tiled=True)
    owners_hit = (requested[None, :] == owner_index[:, None]).astype(BF)
    dense = jnp.einsum("ot,tslc->oslc", owners_hit, returned, preferred_element_type=F32).astype(BF)
    parts = lax.all_to_all(dense, "branch", split_axis=0, concat_axis=0, tiled=True)
    trunk_grad = jnp.sum(parts.astype(F32), axis=0)[None, None]
    kv_grad = jnp.swapaxes(own_part + from_next.astype(F32), 0, 1)[None]
    return (attended[None], query_grad[None], kv_grad, trunk_grad)


def solution(mesh):
    return jax.shard_map(
        on_device,
        mesh=mesh,
        in_specs=(
            P("trunk", "branch", None),
            P("trunk", "branch", None, None),
            P("trunk", "branch", None),
            P("trunk", "branch", None, None, None),
            P("trunk", "branch"),
            P("trunk", None),
            P("trunk", "branch", None),
        ),
        out_specs=(
            P("trunk", "branch", None),
            P("trunk", "branch", None),
            P("trunk", "branch", None, None),
            P("trunk", "branch", None, None, None),
        ),
        check_vma=False,
    )
```

time: 185 us -> 66.5 us (0.36)
  waiting for transfers between devices: 64.8 us -> 15.9 us
  blocking collectives: 31.9 us -> 7.81 us
  matrix products: 22.5 us -> 0.62 us
  local copies, waits for them, and re-layouts: 20.5 us -> 5.58 us
  between operations: 14.5 us -> 0.78 us
  other arithmetic: 10.6 us -> 1.47 us
  Pallas kernels: 0 us -> 8.7 us
  starting transfers between devices: 19.6 us -> 25 us
    reduce_scatter x1 -> x0, waiting for transfers between devices: 56.3 us -> none  [on_device(): mine = lax.psum_scatter(dense, 'branch', scatter_dimension=0, tiled=True)]
    all_gather x1 -> x0, blocking collectives: 31.9 us -> none  [on_device(): piece = lax.all_gather(own_segment, 'branch', axis=0, tiled=True)]
    dot_general x22 -> x2, matrix products: 19.3 us -> 0.62 us  [the longest x1 0.33 us: on_device(): jnp.einsum('ot,tslc->oslc', owners_hit, returned, preferred_element_type=...]
    concatenate x8 -> x0, local copies, waits for them, and re-layouts: 10.2 us -> none  [the longest x4 7.27 us: attend_block(): attended = jnp.concatenate(outputs, axis=1).astype(jnp.bfloat16)]
    pallas_call x0 -> x1, Pallas kernels: none -> 8.7 us  [attend(): pl.pallas_call(attend_kernel, grid=(heads,), in_specs=[pl.BlockSpec(memor...]
    all_to_all x0 -> x1, blocking collectives: none -> 7.81 us  [on_device(): lax.all_to_all(ancestors[0, 0], 'trunk', split_axis=0, concat_axis=0, til...]
    all_to_all x1 -> x2, waiting for transfers between devices: 0.01 us -> 7.37 us  [the longest x1 6.03 us: on_device(): lax.all_to_all(dense, 'branch', split_axis=0, concat_axis=0, tiled=True)]
    all_to_all x1 -> x2, starting transfers between devices: 4.24 us -> 9.57 us  [the longest x1 5.97 us: on_device(): lax.all_to_all(copies, 'branch', split_axis=0, concat_axis=0, tiled=True)]
  transfers between devices with their start and end apart: 7 -> 7, of which waited for: 4 -> 5; matrix products, arithmetic and copies ran while one was open for 8% -> 6% of each run, Pallas kernels for 0% -> 0%
where the time goes in v1:
time: 66.5 us; the launch traced here: 65.8 us
  starting transfers between devices  25 us (38%)
  waiting for transfers between devices  15.9 us (24%)
  Pallas kernels  8.7 us (13%)
  blocking collectives  7.81 us (12%)
  local copies, waits for them, and re-layouts  5.58 us (8%)
  other arithmetic  1.47 us (2%)
  between operations  0.78 us (1%)
    pallas_call x1, Pallas kernels, attend(): pl.pallas_call(attend_kernel, grid=(heads,), in_specs=[pl.BlockSpec(memor...  8.7 us
    ppermute x3, starting transfers between devices, shift(): return lax.ppermute(block, axis, route)  8.6 us
    all_to_all x1, blocking collectives, on_device(): lax.all_to_all(ancestors[0, 0], 'trunk', split_axis=0, concat_axis=0, til...  7.81 us
    all_to_all x1, waiting for transfers between devices, on_device(): lax.all_to_all(dense, 'branch', split_axis=0, concat_axis=0, tiled=True)  6.03 us
    all_to_all x1, starting transfers between devices, on_device(): lax.all_to_all(copies, 'branch', split_axis=0, concat_axis=0, tiled=True)  5.97 us
    all_to_all x1, waiting for transfers between devices, on_device(): lax.all_to_all(picked, 'trunk', split_axis=0, concat_axis=0, tiled=True)  3.98 us
    all_to_all x1, starting transfers between devices, on_device(): lax.all_to_all(dense, 'branch', split_axis=0, concat_axis=0, tiled=True)  3.6 us
    all_to_all x1, starting transfers between devices, on_device(): lax.all_to_all(trunk_part, 'trunk', split_axis=0, concat_axis=0, tiled=True)  3.47 us
  transfers between devices with their start and end apart: 7, of which 5 were waited for; matrix products, arithmetic and copies ran while one was open for 6% of the time, Pallas kernels for 0%

profile of v1, /device:TPU:0, one launch (start us, length us, event | category | flops | bytes accessed | tf_op | source)
XLA Modules:
  0.0 65.8 jit_solution(8273138475993502625)
XLA Ops:
  0.6 0.0 copy-start.5
  0.6 0.6 copy-done.5
  1.3 0.1 copy.20
  1.4 7.8 %all_to_all.29 = s32[4,1,1]{2,1,0:T(1,128)S(1)} all-to-all(s32[4,1,1]{2,1,0:T(1,128)S(1)} %copy.20), channel_id=1, replica_groups=mesh['trunk'=4,'branch'=8] {'trunk'}, dimensions={0} | all-to-all | bytes 32 | tf_op jit(solution)/shard_map/all_to_all | solution.py:127
  9.2 1.5 %broadcast_in_dim.24 = bf16[8,2,16,512]{3,2,1,0:T(8,128)(2,1)} broadcast(bf16[2,16,512]{2,1,0:T(8,128)(2,1)} %bitcast.35), dimensions={1,2,3} | broadcast | bytes 294912 | tf_op jit(solution)/shard_map/broadcast_in_dim | solution.py:129
  10.7 0.0 copy-start.7
  10.7 0.0 copy-start.4
  10.7 6.0 %all-to-all-start.1 = ((bf16[8,2,16,512]{3,2,1,0:T(8,128)(2,1)}), bf16[8,2,16,512]{3,2,1,0:T(8,128)(2,1)S(1)}, u32[]{:S(2)}, u32[]{:S(2)}) async-start(bf16[8,2,16,512]{3,2,1,0:T(8,128)(2,1)} %broadcast_in_dim.24), calls=%async_computation.1 | async-start | bytes 524288 | tf_op jit(solution)/shard_map/all_to_all | solution.py:130
  16.6 0.0 copy-done.7
  16.7 3.9 %collective-permute-start = (s32[128]{0:T(128)S(1)}, s32[128]{0:T(128)S(1)}, u32[]{:S(2)}, u32[]{:S(2)}) collective-permute-start(s32[128]{0:T(128)S(1)} %get-tuple-element.27), channel_id=1, source_target_pairs={{0,1},{1,2},{2,3},{3,4},{4,5},{5,6},{6,7},{8,9},{9,10},{10,11},{11... | collective-permute-start | bytes 1544 | tf_op jit(solution)/shard_map/ppermute | solution.py:22
  20.6 0.0 copy-done.4
  20.6 0.0 copy-start
  20.6 3.4 %collective-permute-start.1 = (bf16[128,1024]{1,0:T(8,128)(2,1)S(1)}, bf16[128,1024]{1,0:T(8,128)(2,1)S(1)}, u32[]{:S(2)}, u32[]{:S(2)}) collective-permute-start(bf16[128,1024]{1,0:T(8,128)(2,1)S(1)} %bitcast.28), channel_id=1, source_target_pairs={{0,1},{1,2},{2,3},{3,4},{4,5},{5,6},{6,7},{8,9},{9,10},{10,11},{11... | collective-permute-start | bytes 786440 | tf_op jit(solution)/shard_map/ppermute | solution.py:22
  24.0 0.2 reduce
  24.2 1.3 %all-to-all-done.1 = bf16[8,2,16,512]{3,2,1,0:T(8,128)(2,1)S(1)} async-done(((bf16[8,2,16,512]{3,2,1,0:T(8,128)(2,1)}), bf16[8,2,16,512]{3,2,1,0:T(8,128)(2,1)S(1)}, u32[]{:S(2)}, u32[]{:S(2)}) %all-to-all-start.1) | async-done | bytes 262176 | tf_op jit(solution)/shard_map/all_to_all | solution.py:130
  25.5 0.3 fusion
  25.8 0.7 %copy.34 = bf16[4,2,16,512]{3,2,1,0:T(8,128)(2,1)} copy(bf16[4,2,16,512]{3,0,2,1:T(4,128)(2,1)S(1)} %fusion) | data formatting | bytes 262144 | tf_op jit(solution)/shard_map/tn,nslc->tslc/dot_general | solution.py:133
  26.5 0.0 copy-done
  26.5 3.3 %all-to-all-start.2 = ((bf16[4,2,16,512]{3,2,1,0:T(8,128)(2,1)}), bf16[4,2,16,512]{3,2,1,0:T(8,128)(2,1)S(1)}, u32[]{:S(2)}, u32[]{:S(2)}) async-start(bf16[4,2,16,512]{3,2,1,0:T(8,128)(2,1)} %copy.34), calls=%async_computation.2 | async-start | bytes 262144 | tf_op jit(solution)/shard_map/all_to_all | solution.py:134
  29.9 0.0 collective-permute-done
  29.9 0.6 pad_add_fusion.tags_ref
  30.4 0.0 collective-permute-done.1.ek_ref.ev_ref
  30.4 0.0 copy-start.1
  30.4 4.0 %all-to-all-done.2.trunk_ref = bf16[4,2,16,512]{3,2,1,0:T(8,128)(2,1)S(1)} async-done(((bf16[4,2,16,512]{3,2,1,0:T(8,128)(2,1)}), bf16[4,2,16,512]{3,2,1,0:T(8,128)(2,1)S(1)}, u32[]{:S(2)}, u32[]{:S(2)}) %all-to-all-start.2) | async-done | bytes 131104 | tf_op jit(solution)/shard_map/all_to_all | solution.py:134
  34.4 0.0 copy-start.2
  34.4 0.0 copy-done.1
  34.4 0.6 copy-done.2
  35.1 8.7 %attend.1 = (bf16[128,4096]{1,0:T(8,128)(2,1)}, bf16[128,4096]{1,0:T(8,128)(2,1)}, bf16[4,2,16,512]{3,2,1,0:T(8,128)(2,1)}, bf16[2,128,512]{2,1,0:T(8,128)(2,1)}, f32[2,128,512]{2,1,0:T(8,128)}) custom-call(s32[16]{0:T(128)} %bitcast.36, s32[2,128]{1,0:T(2,128)} %pad_add_fusion.tags_ref, bf16[128,4096]{1,0:T(8,128)(2,1)} %bitcast.31, ...), custom_call_target="tpu_custom_call" | custom-call | tf_op jit(solution)/shard_map/attend/pallas_call | solution.py:102
  43.8 0.0 copy-start.6
  43.8 3.5 %all-to-all-start.3 = ((bf16[4,2,16,512]{3,2,1,0:T(8,128)(2,1)}), bf16[4,2,16,512]{3,2,1,0:T(8,128)(2,1)S(1)}, u32[]{:S(2)}, u32[]{:S(2)}) async-start(bf16[4,2,16,512]{3,2,1,0:T(8,128)(2,1)} %get-tuple-element.13), calls=%async_computation.3 | async-start | bytes 262144 | tf_op jit(solution)/shard_map/all_to_all | solution.py:143
  47.2 0.0 copy-done.6
  47.3 1.3 %collective-permute-start.2 = (bf16[2,128,512]{2,1,0:T(8,128)(2,1)S(1)}, bf16[2,128,512]{2,1,0:T(8,128)(2,1)S(1)}, u32[]{:S(2)}, u32[]{:S(2)}) collective-permute-start(bf16[2,128,512]{2,1,0:T(8,128)(2,1)S(1)} %copy-done.6), channel_id=1, source_target_pairs={{1,0},{2,1},{3,2},{4,3},{5,4},{6,5},{7,6},{9,8},{10,9},{11,10},{12... | collective-permute-start | bytes 786440 | tf_op jit(solution)/shard_map/ppermute | solution.py:22
  48.6 3.3 %all-to-all-done.3 = bf16[4,2,16,512]{3,2,1,0:T(8,128)(2,1)S(1)} async-done(((bf16[4,2,16,512]{3,2,1,0:T(8,128)(2,1)}), bf16[4,2,16,512]{3,2,1,0:T(8,128)(2,1)S(1)}, u32[]{:S(2)}, u32[]{:S(2)}) %all-to-all-start.3) | async-done | bytes 131104 | tf_op jit(solution)/shard_map/all_to_all | solution.py:143
  51.8 0.3 convolution_convert_fusion
  52.2 0.0 copy-start.3
  52.2 0.8 %copy.24 = bf16[8,2,16,512]{3,2,1,0:T(8,128)(2,1)} copy(bf16[8,2,16,512]{3,0,2,1:T(8,128)(2,1)S(1)} %convolution_convert_fusion) | data formatting | bytes 524288 | tf_op jit(solution)/shard_map/convert_element_type | solution.py:145
  52.9 3.6 %all-to-all-start.4 = ((bf16[8,2,16,512]{3,2,1,0:T(8,128)(2,1)}), bf16[8,2,16,512]{3,2,1,0:T(8,128)(2,1)S(1)}, u32[]{:S(2)}, u32[]{:S(2)}) async-start(bf16[8,2,16,512]{3,2,1,0:T(8,128)(2,1)} %copy.24), calls=%async_computation.4 | async-start | bytes 524288 | tf_op jit(solution)/shard_map/all_to_all | solution.py:146
  56.5 1.3 %collective-permute-done.2 = bf16[2,128,512]{2,1,0:T(8,128)(2,1)S(1)} collective-permute-done((bf16[2,128,512]{2,1,0:T(8,128)(2,1)S(1)}, bf16[2,128,512]{2,1,0:T(8,128)(2,1)S(1)}, u32[]{:S(2)}, u32[]{:S(2)}) %collective-permute-start.2) | collective-permute-done | bytes 262176 | tf_op jit(solution)/shard_map/ppermute | solution.py:22
  57.8 0.0 copy-done.3
  57.8 0.1 add_bitcast_fusion
  57.9 1.2 %copy.25 = f32[1,128,2,512]{3,2,1,0:T(2,128)} copy(f32[1,128,2,512]{3,1,2,0:T(8,128)S(1)} %add_bitcast_fusion) | data formatting | bytes 1048576
  59.1 6.0 %all-to-all-done.4 = bf16[8,2,16,512]{3,2,1,0:T(8,128)(2,1)S(1)} async-done(((bf16[8,2,16,512]{3,2,1,0:T(8,128)(2,1)}), bf16[8,2,16,512]{3,2,1,0:T(8,128)(2,1)S(1)}, u32[]{:S(2)}, u32[]{:S(2)}) %all-to-all-start.4) | async-done | bytes 262176 | tf_op jit(solution)/shard_map/all_to_all | solution.py:146
  65.1 0.7 %convert_reduce_fusion = f32[2,16,512]{2,1,0:T(8,128)} fusion(bf16[8,2,16,512]{3,2,1,0:T(8,128)(2,1)S(1)} %all-to-all-done.4), kind=kLoop, calls=%fused_computation.1 | loop fusion | flops 245760 | bytes 327680 | tf_op jit(solution)/shard_map/reduce_sum | solution.py:147
  (2 shorter events, 0.0 us)
Async XLA Ops:
  0.6 0.7 copy-start.5
  10.7 6.0 %copy-start.7 = (s32[1,128]{1,0:T(1,128)S(1)}, s32[1,128]{1,0:T(1,128)}, u32[]{:S(2)}) copy-start(s32[1,128]{1,0:T(1,128)} %param.11) | copy-start | bytes 1540
  10.7 9.9 %copy-start.4 = (bf16[1,128,2,512]{3,2,1,0:T(2,128)(2,1)S(1)}, bf16[1,128,2,512]{3,2,1,0:T(2,128)(2,1)}, u32[]{:S(2)}) copy-start(bf16[1,128,2,512]{3,2,1,0:T(2,128)(2,1)} %param.8) | copy-start | bytes 786436
  10.7 14.9 %all-to-all-start.1 = ((bf16[8,2,16,512]{3,2,1,0:T(8,128)(2,1)}), bf16[8,2,16,512]{3,2,1,0:T(8,128)(2,1)S(1)}, u32[]{:S(2)}, u32[]{:S(2)}) async-start(bf16[8,2,16,512]{3,2,1,0:T(8,128)(2,1)} %broadcast_in_dim.24), calls=%async_computation.1 | async-start | bytes 524288 | tf_op jit(solution)/shard_map/all_to_all | solution.py:130
  16.7 13.2 %collective-permute-start = (s32[128]{0:T(128)S(1)}, s32[128]{0:T(128)S(1)}, u32[]{:S(2)}, u32[]{:S(2)}) collective-permute-start(s32[128]{0:T(128)S(1)} %get-tuple-element.27), channel_id=1, source_target_pairs={{0,1},{1,2},{2,3},{3,4},{4,5},{5,6},{6,7},{8,9},{9,10},{10,11},{11... | collective-permute-start | bytes 1544 | tf_op jit(solution)/shard_map/ppermute | solution.py:22
  20.6 5.9 %copy-start = (bf16[16,8,2,512]{3,1,2,0:T(8,128)(2,1)}, bf16[16,8,2,512]{3,1,2,0:T(8,128)(2,1)S(1)}, u32[]{:S(2)}) copy-start(bf16[16,8,2,512]{3,1,2,0:T(8,128)(2,1)S(1)} %copy.28) | copy-start | bytes 786436
  20.6 9.8 %collective-permute-start.1 = (bf16[128,1024]{1,0:T(8,128)(2,1)S(1)}, bf16[128,1024]{1,0:T(8,128)(2,1)S(1)}, u32[]{:S(2)}, u32[]{:S(2)}) collective-permute-start(bf16[128,1024]{1,0:T(8,128)(2,1)S(1)} %bitcast.28), channel_id=1, source_target_pairs={{0,1},{1,2},{2,3},{3,4},{4,5},{5,6},{6,7},{8,9},{9,10},{10,11},{11... | collective-permute-start | bytes 786440 | tf_op jit(solution)/shard_map/ppermute | solution.py:22
  26.5 7.9 %all-to-all-start.2 = ((bf16[4,2,16,512]{3,2,1,0:T(8,128)(2,1)}), bf16[4,2,16,512]{3,2,1,0:T(8,128)(2,1)S(1)}, u32[]{:S(2)}, u32[]{:S(2)}) async-start(bf16[4,2,16,512]{3,2,1,0:T(8,128)(2,1)} %copy.34), calls=%async_computation.2 | async-start | bytes 262144 | tf_op jit(solution)/shard_map/all_to_all | solution.py:134
  30.4 4.0 %copy-start.1 = (bf16[128,1024]{1,0:T(8,128)(2,1)}, bf16[128,1024]{1,0:T(8,128)(2,1)S(1)}, u32[]{:S(2)}) copy-start(bf16[128,1024]{1,0:T(8,128)(2,1)S(1)} %collective-permute-done.1.ek_ref.ev_ref) | copy-start | bytes 786436
  34.4 0.6 copy-start.2
  43.8 3.5 %copy-start.6 = (bf16[2,128,512]{2,1,0:T(8,128)(2,1)S(1)}, bf16[2,128,512]{2,1,0:T(8,128)(2,1)}, u32[]{:S(2)}) copy-start(bf16[2,128,512]{2,1,0:T(8,128)(2,1)} %get-tuple-element.12) | copy-start | bytes 786436
  43.8 8.0 %all-to-all-start.3 = ((bf16[4,2,16,512]{3,2,1,0:T(8,128)(2,1)}), bf16[4,2,16,512]{3,2,1,0:T(8,128)(2,1)S(1)}, u32[]{:S(2)}, u32[]{:S(2)}) async-start(bf16[4,2,16,512]{3,2,1,0:T(8,128)(2,1)} %get-tuple-element.13), calls=%async_computation.3 | async-start | bytes 262144 | tf_op jit(solution)/shard_map/all_to_all | solution.py:143
  47.3 10.6 %collective-permute-start.2 = (bf16[2,128,512]{2,1,0:T(8,128)(2,1)S(1)}, bf16[2,128,512]{2,1,0:T(8,128)(2,1)S(1)}, u32[]{:S(2)}, u32[]{:S(2)}) collective-permute-start(bf16[2,128,512]{2,1,0:T(8,128)(2,1)S(1)} %copy-done.6), channel_id=1, source_target_pairs={{1,0},{2,1},{3,2},{4,3},{5,4},{6,5},{7,6},{9,8},{10,9},{11,10},{12... | collective-permute-start | bytes 786440 | tf_op jit(solution)/shard_map/ppermute | solution.py:22
  52.2 5.7 %copy-start.3 = (f32[2,128,512]{2,1,0:T(8,128)S(1)}, f32[2,128,512]{2,1,0:T(8,128)}, u32[]{:S(2)}) copy-start(f32[2,128,512]{2,1,0:T(8,128)} %get-tuple-element.11) | copy-start | bytes 1572868
  52.9 12.2 %all-to-all-start.4 = ((bf16[8,2,16,512]{3,2,1,0:T(8,128)(2,1)}), bf16[8,2,16,512]{3,2,1,0:T(8,128)(2,1)S(1)}, u32[]{:S(2)}, u32[]{:S(2)}) async-start(bf16[8,2,16,512]{3,2,1,0:T(8,128)(2,1)} %copy.24), calls=%async_computation.4 | async-start | bytes 524288 | tf_op jit(solution)/shard_map/all_to_all | solution.py:146

commit v2 on v1

v2 whole, which is shorter than its diff:
```python
import functools
import math

import jax
import jax.numpy as jnp
from jax import lax
from jax.experimental import pallas as pl
from jax.experimental.pallas import tpu as pltpu
from jax.sharding import PartitionSpec as P


HQ = 32
KVH = 4
DH = 128
GROUP = HQ // KVH
SCALE = 1.0 / math.sqrt(DH)
LOG2E = 1.0 / math.log(2.0)
BF = jnp.bfloat16
F32 = jnp.float32
PACK = 16
GATHER_FIRST = []
SCATTER_FIRST = [1]
VMEM_LIMIT = 24 * 1024 * 1024


def ring(block, axis, distance):
    size = lax.axis_size(axis)
    return lax.ppermute(block, axis, [(i, (i + distance) % size) for i in range(size)])


def swap(block, axis, k):
    if k == 0:
        return block
    return lax.ppermute(block, axis, [(i, i ^ k) for i in range(lax.axis_size(axis))])


def dot(a, b, ca, cb):
    return lax.dot_general(a, b, (((ca,), (cb,)), ((), ())), preferred_element_type=F32)


def head_rows(ref, h):
    first = h * GROUP
    return jnp.concatenate(
        [ref[:, (first + r) * DH : (first + r + 1) * DH] for r in range(GROUP)], axis=0
    )


def tile_heads(x):
    return jnp.concatenate([x] * GROUP, axis=1)


def as_bias(ok):
    return jnp.where(ok, 0.0, -1e30).astype(F32)


def cols(h):
    return slice(h * DH, (h + 1) * DH)


def call(kernel, outs, *args, hbm=0, hbm_outs=0, scratch=(), aliases={}):
    vspec = pl.BlockSpec(memory_space=pltpu.VMEM)
    hspec = pl.BlockSpec(memory_space=pltpu.HBM)
    places = [pltpu.HBM] * hbm + [pltpu.VMEM] * (len(args) - hbm)
    args = [pltpu.with_memory_space_constraint(a, p) for a, p in zip(args, places)]
    shapes = [jax.ShapeDtypeStruct(shape, dtype) for shape, dtype in outs[:hbm_outs]]
    shapes += [pltpu.VMEM(shape, dtype) for shape, dtype in outs[hbm_outs:]]
    return pl.pallas_call(
        kernel,
        in_specs=[hspec] * hbm + [vspec] * (len(args) - hbm),
        out_specs=[hspec] * hbm_outs + [vspec] * (len(outs) - hbm_outs),
        out_shape=shapes,
        scratch_shapes=scratch,
        input_output_aliases=aliases,
        compiler_params=pltpu.CompilerParams(vmem_limit_bytes=VMEM_LIMIT),
        cost_estimate=pl.CostEstimate(flops=10**8, transcendentals=0, bytes_accessed=10**5),
    )(*args)


def join_kernel(a_ref, b_ref, out_ref):
    count = a_ref.shape[0]
    out_ref[:count] = a_ref[...]
    out_ref[count:] = b_ref[...]


def prepare_kernel(
    ids_hbm, reach_hbm, owners_hbm, q_hbm, g_hbm, seg_hbm, kv_ref,
    ids_ref, owners_ref, q_ref, g_ref, seg_ref, payload_ref, tbias_ref, reach_ref, sems,
):
    copies = [
        pltpu.make_async_copy(src, dst, sems.at[i])
        for i, (src, dst) in enumerate(
            (
                (ids_hbm, ids_ref), (reach_hbm, reach_ref), (owners_hbm, owners_ref),
                (seg_hbm, seg_ref), (q_hbm, q_ref), (g_hbm, g_ref),
            )
        )
    ]
    for copy in copies:
        copy.start()
    n = kv_ref.shape[0]
    payload_ref[:n] = kv_ref[...]
    payload_ref[n:] = jnp.zeros((PACK, kv_ref.shape[1]), BF)
    copies[0].wait()
    copies[1].wait()
    ids = ids_ref[...]
    payload_ref[n:, 0:n] = jnp.broadcast_to((ids + 1).astype(F32), (PACK, n)).astype(BF)
    reach_row = jnp.zeros((1, n), jnp.int32)
    for b in range(reach_ref.shape[1]):
        reach_row = jnp.where(ids == b, reach_ref[0:1, b : b + 1], reach_row)
    depths = lax.axis_size("trunk")
    seg_len = tbias_ref.shape[0] // depths
    me = lax.axis_index("trunk")
    for k in range(depths):
        row = as_bias((me ^ k) < reach_row)
        tbias_ref[k * seg_len : (k + 1) * seg_len] = jnp.broadcast_to(row, (seg_len, n))
    for copy in copies[2:]:
        copy.wait()


def scored(keys, values, q_rows, g_rows, bias):
    return dot(keys, q_rows, 1, 1) * (SCALE * LOG2E) + bias, dot(values, g_rows, 1, 1)


def own_kernel(ids_ref, q_ref, g_ref, kv_ref, stats_ref, bias_ref):
    n = q_ref.shape[0]
    heads = stats_ref.shape[0]
    id_cols = jnp.broadcast_to(ids_ref[...].astype(F32), (n, n))
    k_idx = lax.broadcasted_iota(jnp.int32, (n, n), 0)
    q_idx = lax.broadcasted_iota(jnp.int32, (n, n), 1)
    bias_ref[...] = as_bias((id_cols.T == id_cols) & (k_idx <= q_idx))
    bias = tile_heads(bias_ref[...])
    for h in range(heads):
        scores, grad_w = scored(
            kv_ref[:n, cols(h)], kv_ref[:n, cols(h + heads)],
            head_rows(q_ref, h), head_rows(g_ref, h), bias,
        )
        highest = jnp.max(scores, axis=0, keepdims=True)
        expo = jnp.exp2(scores - highest)
        stats_ref[h, 0:1] = highest
        stats_ref[h, 1:2] = jnp.sum(expo, axis=0, keepdims=True)
        stats_ref[h, 2:3] = jnp.sum(expo * grad_w, axis=0, keepdims=True)


def merge(stats_ref, h, scores, grad_w):
    first = stats_ref[h, 0:1]
    highest = jnp.maximum(jnp.max(scores, axis=0, keepdims=True), first)
    expo = jnp.exp2(scores - highest)
    factor = jnp.exp2(first - highest)
    total = jnp.sum(expo, axis=0, keepdims=True) + stats_ref[h, 1:2] * factor
    weighted = jnp.sum(expo * grad_w, axis=0, keepdims=True) + stats_ref[h, 2:3] * factor
    return highest, expo, total, weighted


def earlier_kernel(ids_ref, q_ref, g_ref, kv_ref, stats_ref, merged_ref, bias_ref):
    n = q_ref.shape[0]
    heads = stats_ref.shape[0]
    tag_cols = jnp.broadcast_to(ids_ref[...].astype(F32) + 1.0, (n, n))
    present = (lax.axis_index("branch") > 0).astype(F32)
    earlier_row = kv_ref[n : n + 1, 0:n].astype(F32) * present
    bias_ref[...] = as_bias(jnp.broadcast_to(earlier_row, (n, n)).T == tag_cols)
    bias = tile_heads(bias_ref[...])
    for h in range(heads):
        scores, grad_w = scored(
            kv_ref[:n, cols(h)], kv_ref[:n, cols(h + heads)],
            head_rows(q_ref, h), head_rows(g_ref, h), bias,
        )
        highest, _, total, weighted = merge(stats_ref, h, scores, grad_w)
        merged_ref[h, 0:1] = highest
        merged_ref[h, 1:2] = total
        merged_ref[h, 2:3] = weighted


def trunk_kernel(q_ref, g_ref, stats_ref, tbias_ref, *refs):
    count = len(refs) // 2
    seg_refs, final_ref, dseg_refs = refs[:count], refs[count], refs[count + 1 :]
    seg_len = seg_refs[0].shape[1]
    bias = tile_heads(tbias_ref[...])
    for h in range(stats_ref.shape[0]):
        keys = jnp.concatenate([s[0, :, cols(h)] for s in seg_refs], axis=0)
        values = jnp.concatenate([s[1, :, cols(h)] for s in seg_refs], axis=0)
        q_rows = head_rows(q_ref, h)
        g_rows = head_rows(g_ref, h)
        scores, grad_w = scored(keys, values, q_rows, g_rows, bias)
        highest, expo, total, weighted = merge(stats_ref, h, scores, grad_w)
        inverse = 1.0 / total
        row_mean = weighted * inverse
        weights = expo * inverse
        score_grad = (weights * (grad_w - row_mean)).astype(BF)
        dkey = (dot(score_grad, q_rows, 1, 0) * SCALE).astype(BF)
        dvalue = dot(weights.astype(BF), g_rows, 1, 0).astype(BF)
        for k, ref in enumerate(dseg_refs):
            ref[0, :, cols(h)] = dkey[k * seg_len : (k + 1) * seg_len]
            ref[1, :, cols(h)] = dvalue[k * seg_len : (k + 1) * seg_len]
        final_ref[h, 0:1] = highest
        final_ref[h, 1:2] = inverse
        final_ref[h, 2:3] = row_mean


def finish(final_ref, h, scores, grad_w):
    weights = jnp.exp2(scores - final_ref[h, 0:1]) * final_ref[h, 1:2]
    return weights.astype(BF), (weights * (grad_w - final_ref[h, 2:3])).astype(BF)


def earlier_grad_kernel(q_ref, g_ref, final_ref, kv_ref, bias_ref, dkv_ref):
    n = q_ref.shape[0]
    heads = final_ref.shape[0]
    bias = tile_heads(bias_ref[...])
    for h in range(heads):
        q_rows = head_rows(q_ref, h)
        g_rows = head_rows(g_ref, h)
        scores, grad_w = scored(
            kv_ref[:n, cols(h)], kv_ref[:n, cols(h + heads)], q_rows, g_rows, bias
        )
        weights_bf, score_grad = finish(final_ref, h, scores, grad_w)
        dkv_ref[0, :, cols(h)] = (dot(score_grad, q_rows, 1, 0) * SCALE).astype(BF)
        dkv_ref[1, :, cols(h)] = dot(weights_bf, g_rows, 1, 0).astype(BF)


def rest_kernel(
    *refs, some, aliased
):
    refs = refs[2:] if aliased else refs
    q_ref, g_ref, final_ref, ekv_ref, kv_ref, obias_ref, ebias_ref, tbias_ref = refs[:8]
    seg_refs = refs[8:-6]
    out_hbm, dq_hbm, dkv_ref, out_ref, dq_ref, sems = refs[-6:]
    n = q_ref.shape[0]
    heads = final_ref.shape[0]
    part = GROUP * DH
    bias = tile_heads(jnp.concatenate([obias_ref[...], ebias_ref[...], tbias_ref[...]], axis=0))
    copies = []
    for i, h in enumerate(some):
        keys = jnp.concatenate(
            [kv_ref[:n, cols(h)], ekv_ref[:n, cols(h)]] + [s[0, :, cols(h)] for s in seg_refs],
            axis=0,
        )
        values = jnp.concatenate(
            [kv_ref[:n, cols(h + heads)], ekv_ref[:n, cols(h + heads)]]
            + [s[1, :, cols(h)] for s in seg_refs],
            axis=0,
        )
        q_rows = head_rows(q_ref, h)
        g_rows = head_rows(g_ref, h)
        scores, grad_w = scored(keys, values, q_rows, g_rows, bias)
        weights_bf, score_grad = finish(final_ref, h, scores, grad_w)
        out_t = dot(values, weights_bf, 0, 0)
        dq_t = dot(keys, score_grad, 0, 0) * SCALE
        for r in range(GROUP):
            rows = slice(r * n, (r + 1) * n)
            out_ref[i, :, cols(r)] = out_t[:, rows].T.astype(BF)
            dq_ref[i, :, cols(r)] = dq_t[:, rows].T.astype(BF)
        for which, (src, dst) in enumerate(((out_ref, out_hbm), (dq_ref, dq_hbm))):
            copy = pltpu.make_async_copy(
                src.at[i], dst.at[:, pl.ds(h * part, part)], sems.at[which, i]
            )
            copy.start()
            copies.append(copy)
        dkv_ref[0, :, cols(i)] = dot(score_grad[:n], q_rows, 1, 0) * SCALE
        dkv_ref[1, :, cols(i)] = dot(weights_bf[:n], g_rows, 1, 0)
    for copy in copies:
        copy.wait()


def owner_of(ref):
    owners = ref[...]
    lane = lax.broadcasted_iota(jnp.int32, owners.shape, 1)
    mine = jnp.where(lane == lax.axis_index("trunk"), owners, 0)
    return jnp.sum(mine.astype(F32), axis=1, keepdims=True)


def pick_kernel(near_ref, far_ref, *refs, offsets):
    count = len(refs) // 2
    me = lax.axis_index("branch")
    half = near_ref.shape[0]
    for owner_ref, out_ref in zip(refs[:count], refs[count:]):
        owner = owner_of(owner_ref)
        for which in range(out_ref.shape[0]):
            total = jnp.zeros(out_ref.shape[1:], F32)
            for p, offset in enumerate(offsets):
                ref = near_ref if p < half else far_ref
                hit = owner == (me ^ offset).astype(F32)
                total = jnp.where(hit, ref[p % half, which].astype(F32), total)
            out_ref[which] = total.astype(BF)


def split_kernel(*refs, keeps, sends):
    send_ref, keep_ref = refs[-2:]
    count = (len(refs) - 2) // 2
    me = lax.axis_index("branch")
    owners = [owner_of(ref) for ref in refs[:count]]
    for which in range(keep_ref.shape[1]):
        parts = [ref[which].astype(F32) for ref in refs[count:-2]]
        for out_ref, offsets in ((keep_ref, keeps), (send_ref, sends)):
            for i, offset in enumerate(offsets):
                total = jnp.zeros(parts[0].shape, F32)
                for owner, part in zip(owners, parts):
                    hit = owner == (me ^ offset).astype(F32)
                    total = total + jnp.where(hit, part, 0.0)
                out_ref[i, which] = total.astype(out_ref.dtype)


def fold_kernel(kept_ref, got_ref, *out_refs, places):
    for out_ref, where in zip(out_refs, places):
        for i, p in enumerate(where):
            out_ref[i] = (kept_ref[p] + got_ref[p].astype(F32)).astype(out_ref.dtype)


def combine_kernel(next_ref, *refs):
    out_ref = refs[-1]
    first = 0
    for ref in refs[:-1]:
        some = slice(first, first + ref.shape[2])
        for which in range(out_ref.shape[1]):
            out_ref[:, which, some] = ref[which] + next_ref[which, :, some].astype(F32)
        first += ref.shape[2]


def on_device(queries, keys_values, out_grad, trunk_kv, branch_of, branch_reach, ancestors):
    depths = lax.axis_size("trunk")
    n_branch = lax.axis_size("branch")
    n, width = queries.shape[1:]
    seg_len, kv_width = trunk_kv.shape[3:]
    heads = kv_width // DH
    seg_shape = trunk_kv.shape[2:]
    stats_shape = ((heads, 8, n * GROUP), F32)
    bias_shape = ((n, n), F32)
    tbias_shape = ((depths * seg_len, n), F32)
    assert branch_reach.shape[1] < 256 and n_branch & (n_branch - 1) == 0

    bits = [1 << i for i in range(n_branch.bit_length() - 1)][::-1]
    bits = GATHER_FIRST + [x for x in bits if x not in GATHER_FIRST]
    offsets, bit = [0], bits[0]
    far = swap(trunk_kv[0], "branch", bit)
    offsets = offsets + [bit ^ o for o in offsets]
    own_kv = keys_values[0].reshape(n, 2 * kv_width)
    ids, own_owners, q, g, near, payload, tbias = call(
        prepare_kernel,
        [
            ((1, n), jnp.int32), ((1, depths), jnp.int32), ((n, width), BF), ((n, width), BF),
            ((1,) + seg_shape, BF), ((n + PACK, 2 * kv_width), BF), tbias_shape,
        ],
        branch_of, branch_reach, ancestors[0], queries[0], out_grad[0], trunk_kv[0], own_kv,
        hbm=6,
        scratch=[pltpu.VMEM(branch_reach.shape, jnp.int32), pltpu.SemaphoreType.DMA((6,))],
    )
    earlier = ring(payload, "branch", 1)
    owners = [own_owners]
    for k in range(1, depths):
        owners.append(swap(own_owners, "trunk", k))
    for step, bit in enumerate(bits[1:], 1):
        (near,) = call(join_kernel, [((2 * near.shape[0],) + seg_shape, BF)], near, far)
        far = swap(near, "branch", bit)
        offsets = offsets + [bit ^ o for o in offsets]
    stats0, obias = call(own_kernel, [stats_shape, bias_shape], ids, q, g, payload)
    stats1, ebias = call(earlier_kernel, [stats_shape, bias_shape], ids, q, g, earlier, stats0)
    picked = call(
        functools.partial(pick_kernel, offsets=offsets), [(seg_shape, BF)] * depths,
        near, far, *owners,
    )
    segs = [picked[0]]
    for k in range(1, depths):
        segs.append(swap(picked[k], "trunk", k))
    final, *dsegs = call(
        trunk_kernel, [stats_shape] + [(seg_shape, BF)] * depths,
        q, g, stats1, tbias, *segs,
    )
    returned = [dsegs[0]]
    for k in range(1, depths):
        returned.append(swap(dsegs[k], "trunk", k))
    (earlier_part,) = call(
        earlier_grad_kernel, [((2, n, kv_width), BF)],
        q, g, final, earlier, ebias,
    )
    from_next = ring(earlier_part, "branch", -1)
    keeps = list(range(n_branch))
    order = [1 << i for i in range(n_branch.bit_length() - 1)]
    order = SCATTER_FIRST + [x for x in order if x not in SCATTER_FIRST]
    order = [x for x in order if x < n_branch]
    for step, bit in enumerate(order):
        places = [[i for i, o in enumerate(keeps) if not o & bit]]
        places += [[i for i, o in enumerate(keeps) if o & bit]]
        sends = [keeps[i] for i in places[1]]
        keeps = [keeps[i] for i in places[0]]
        sends = [o ^ bit for o in sends]
        assert sends == keeps
        half = (len(keeps),) + seg_shape
        outs = [(half, BF), (half, F32)]
        if step == 0:
            send, kept = call(
                functools.partial(split_kernel, keeps=keeps, sends=[o ^ bit for o in keeps]),
                outs, *owners, *returned,
            )
        else:
            send, kept = call(functools.partial(fold_kernel, places=places[::-1]), outs, kept, got)
        got = swap(send, "branch", bit)
    (trunk_grad,) = call(
        functools.partial(fold_kernel, places=[[0]]),
        [((1,) + seg_shape, F32)], kept, got,
    )
    own_parts, outputs = [], []
    halves = 2
    for part in range(halves):
        some = list(range(heads))[part * heads // halves : (part + 1) * heads // halves]
        *outputs, own_part = call(
            functools.partial(rest_kernel, some=some, aliased=part > 0),
            [((n, width), BF), ((n, width), BF), ((2, n, len(some) * DH), F32)],
            *outputs, q, g, final, earlier, payload, obias, ebias, tbias, *segs,
            hbm=len(outputs), hbm_outs=2, aliases={i: i for i in range(len(outputs))},
            scratch=[
                pltpu.VMEM((len(some), n, width // heads), BF),
                pltpu.VMEM((len(some), n, width // heads), BF),
                pltpu.SemaphoreType.DMA((2, len(some))),
            ],
        )
        own_parts.append(own_part)
    attended, query_grad = outputs
    (kv_grad,) = call(combine_kernel, [((n, 2, kv_width), F32)], from_next, *own_parts)
    kv_grad = kv_grad[None]
    trunk_grad = trunk_grad[None]
    return (attended[None], query_grad[None], kv_grad, trunk_grad)


def solution(mesh):
    return jax.shard_map(
        on_device,
        mesh=mesh,
        in_specs=(
            P("trunk", "branch", None),
            P("trunk", "branch", None, None),
            P("trunk", "branch", None),
            P("trunk", "branch", None, None, None),
            P("trunk", "branch"),
            P("trunk", None),
            P("trunk", "branch", None),
        ),
        out_specs=(
            P("trunk", "branch", None),
            P("trunk", "branch", None),
            P("trunk", "branch", None, None),
            P("trunk", "branch", None, None, None),
        ),
        check_vma=False,
    )
```

time: 66.5 us -> 60.6 us (0.911)
  blocking collectives: 7.81 us -> 0 us
  waiting for transfers between devices: 15.9 us -> 21.3 us
  Pallas kernels: 8.7 us -> 13.3 us
  local copies, waits for them, and re-layouts: 5.58 us -> 2.41 us
  starting transfers between devices: 25 us -> 22.6 us
  other arithmetic: 1.47 us -> 0 us
    ppermute x3 -> x17, waiting for transfers between devices: 1.27 us -> 21.3 us  [the longest x15 21.3 us: swap(): lax.ppermute(block, axis, [(i, i ^ k) for i in range(lax.axis_size(axis))])]
    all_to_all x4 -> x0, starting transfers between devices: 16.4 us -> none  [the longest x1 5.97 us: on_device(): lax.all_to_all(copies, 'branch', split_axis=0, concat_axis=0, tiled=True)]
    all_to_all x4 -> x0, waiting for transfers between devices: 14.6 us -> none  [the longest x1 6.03 us: on_device(): lax.all_to_all(dense, 'branch', split_axis=0, concat_axis=0, tiled=True)]
    ppermute x3 -> x17, starting transfers between devices: 8.6 us -> 22.6 us  [the longest x15 17.6 us: swap(): lax.ppermute(block, axis, [(i, i ^ k) for i in range(lax.axis_size(axis))])]
    all_to_all x1 -> x0, blocking collectives: 7.81 us -> none  [on_device(): lax.all_to_all(ancestors[0, 0], 'trunk', split_axis=0, concat_axis=0, til...]
    pallas_call x1 -> x15, Pallas kernels: 8.7 us -> 13.3 us  [call(): pl.pallas_call(kernel, in_specs=[hspec] * hbm + [vspec] * (len(args) - hb...]
    broadcast_in_dim x1 -> x0, local copies, waits for them, and re-layouts: 1.49 us -> none  [on_device(): copies = jnp.broadcast_to(own_segment, (n_branch,) + own_segment.shape[1:])]
    convert_element_type x1 -> x0, local copies, waits for them, and re-layouts: 0.78 us -> none  [on_device(): jnp.einsum('ot,tslc->oslc', owners_hit, returned, preferred_element_type=...]
  transfers between devices with their start and end apart: 7 -> 17, of which waited for: 5 -> 7; matrix products, arithmetic and copies ran while one was open for 6% -> 1% of each run, Pallas kernels for 0% -> 16%
where the time goes in v2:
time: 60.6 us; the launch traced here: 60.4 us
  starting transfers between devices  22.6 us (37%)
  waiting for transfers between devices  21.3 us (35%)
  Pallas kernels  13.3 us (22%)
  local copies, waits for them, and re-layouts  2.41 us (4%)
  between operations  0.77 us (1%)
    ppermute x15, waiting for transfers between devices, swap(): lax.ppermute(block, axis, [(i, i ^ k) for i in range(lax.axis_size(axis))])  21.3 us
    ppermute x15, starting transfers between devices, swap(): lax.ppermute(block, axis, [(i, i ^ k) for i in range(lax.axis_size(axis))])  17.6 us
    pallas_call x15, Pallas kernels, call(): pl.pallas_call(kernel, in_specs=[hspec] * hbm + [vspec] * (len(args) - hb...  13.3 us
    ppermute x2, starting transfers between devices, ring(): lax.ppermute(block, axis, [(i, (i + distance) % size) for i in range(size)])  5.05 us
    unnamed x5, local copies, waits for them, and re-layouts  2.41 us
  transfers between devices with their start and end apart: 17, of which 7 were waited for; matrix products, arithmetic and copies ran while one was open for 1% of the time, Pallas kernels for 16%

profile of v2, /device:TPU:0, one launch (start us, length us, event | category | flops | bytes accessed | tf_op | source)
XLA Modules:
  0.0 60.4 jit_solution(3721100107437296139)
XLA Ops:
  0.6 1.0 %copy.13 = bf16[16,8,2,512]{3,1,2,0:T(8,128)(2,1)S(1)} copy(bf16[16,8,2,512]{3,2,1,0:T(2,128)(2,1)} %bitcast.18) | data formatting | bytes 524288
  1.6 0.0 copy-start
  1.6 1.7 %shard_map.102 = (s32[1,128]{1,0:T(1,128)S(1)}, s32[1,4]{1,0:T(1,128)S(1)}, bf16[128,4096]{1,0:T(8,128)(2,1)S(1)}, bf16[128,4096]{1,0:T(8,128)(2,1)S(1)}, bf16[1...) custom-call(s32[1,128]{1,0:T(1,128)} %ids_hbm.1, s32[1,16]{1,0:T(1,128)} %reach_hbm.1, ...), custom_call_target="tpu_custom_call" | custom-call | flops 100000000 | bytes 100000 | tf_op jit(solution)/shard_map/pallas_call | solution.py:67
  3.3 3.0 %collective-permute-start = (bf16[144,1024]{1,0:T(8,128)(2,1)S(1)}, bf16[144,1024]{1,0:T(8,128)(2,1)S(1)}, u32[]{:S(2)}, u32[]{:S(2)}) collective-permute-start(bf16[144,1024]{1,0:T(8,128)(2,1)S(1)} %get-tuple-element.39.kv_ref.refs_4_.refs_6_), channel_id=1, source_target_pairs={{0,1},{1,2},{2,3},{3,4},{4,5},{5,6},{6,7},{7,0},{8,9},{9,10},{10,1... | collective-permute-start | bytes 884744 | tf_op jit(solution)/shard_map/ppermute | solution.py:28
  6.4 0.0 copy-done
  6.4 2.6 %collective-permute-start.1 = (bf16[1,2,16,512]{3,2,1,0:T(8,128)(2,1)S(1)}, bf16[1,2,16,512]{3,2,1,0:T(8,128)(2,1)S(1)}, u32[]{:S(2)}, u32[]{:S(2)}) collective-permute-start(bf16[1,2,16,512]{3,2,1,0:T(8,128)(2,1)S(1)} %bitcast.20), channel_id=1, source_target_pairs={{0,4},{1,5},{2,6},{3,7},{4,0},{5,1},{6,2},{7,3},{8,12},{9,13},{10,... | collective-permute-start | bytes 98312 | tf_op jit(solution)/shard_map/ppermute | solution.py:34
  8.9 2.2 %collective-permute-done.1.b_ref = bf16[1,2,16,512]{3,2,1,0:T(8,128)(2,1)S(1)} collective-permute-done((bf16[1,2,16,512]{3,2,1,0:T(8,128)(2,1)S(1)}, bf16[1,2,16,512]{3,2,1,0:T(8,128)(2,1)S(1)}, u32[]{:S(2)}, u32[]{:S(2)}) %collective-permute-start.1) | collective-permute-done | bytes 32800 | tf_op jit(solution)/shard_map/ppermute | solution.py:34
  11.2 1.6 %collective-permute-start.2 = (bf16[2,2,16,512]{3,2,1,0:T(8,128)(2,1)S(1)}, bf16[2,2,16,512]{3,2,1,0:T(8,128)(2,1)S(1)}, u32[]{:S(2)}, u32[]{:S(2)}) collective-permute-start(bf16[2,2,16,512]{3,2,1,0:T(8,128)(2,1)S(1)} %shard_map.105.a_ref), channel_id=1, source_target_pairs={{0,2},{1,3},{2,0},{3,1},{4,6},{5,7},{6,4},{7,5},{8,10},{9,11},{10,... | collective-permute-start | bytes 196616 | tf_op jit(solution)/shard_map/ppermute | solution.py:34
  12.8 2.7 %collective-permute-done.2.b_ref = bf16[2,2,16,512]{3,2,1,0:T(8,128)(2,1)S(1)} collective-permute-done((bf16[2,2,16,512]{3,2,1,0:T(8,128)(2,1)S(1)}, bf16[2,2,16,512]{3,2,1,0:T(8,128)(2,1)S(1)}, u32[]{:S(2)}, u32[]{:S(2)}) %collective-permute-start.2) | collective-permute-done | bytes 65568 | tf_op jit(solution)/shard_map/ppermute | solution.py:34
  15.5 7.3 %collective-permute-start.3 = (bf16[4,2,16,512]{3,2,1,0:T(8,128)(2,1)S(1)}, bf16[4,2,16,512]{3,2,1,0:T(8,128)(2,1)S(1)}, u32[]{:S(2)}, u32[]{:S(2)}) collective-permute-start(bf16[4,2,16,512]{3,2,1,0:T(8,128)(2,1)S(1)} %shard_map.106.near_ref), channel_id=1, source_target_pairs={{0,1},{1,0},{2,3},{3,2},{4,5},{5,4},{6,7},{7,6},{8,9},{9,8},{10,11... | collective-permute-start | bytes 393224 | tf_op jit(solution)/shard_map/ppermute | solution.py:34
  22.7 0.0 collective-permute-start.4
  22.7 1.5 %collective-permute-start.5 = (s32[1,4]{1,0:T(1,128)S(1)}, s32[1,4]{1,0:T(1,128)S(1)}, u32[]{:S(2)}, u32[]{:S(2)}) collective-permute-start(s32[1,4]{1,0:T(1,128)S(1)} %get-tuple-element.44.refs_0_), channel_id=1, source_target_pairs={{0,16},{8,24},{16,0},{24,8},{1,17},{9,25},{17,1},{25,9},{2,18},{10... | collective-permute-start | bytes 56 | tf_op jit(solution)/shard_map/ppermute | solution.py:34
  24.2 0.4 collective-permute-start.6
  24.6 0.0 collective-permute-done.4.refs_1_
  24.6 1.7 %collective-permute-done.5.refs_2_ = s32[1,4]{1,0:T(1,128)S(1)} collective-permute-done((s32[1,4]{1,0:T(1,128)S(1)}, s32[1,4]{1,0:T(1,128)S(1)}, u32[]{:S(2)}, u32[]{:S(2)}) %collective-permute-start.5) | collective-permute-done | bytes 48 | tf_op jit(solution)/shard_map/ppermute | solution.py:34
  26.3 0.9 %collective-permute-done.6.refs_3_ = s32[1,4]{1,0:T(1,128)S(1)} collective-permute-done((s32[1,4]{1,0:T(1,128)S(1)}, s32[1,4]{1,0:T(1,128)S(1)}, u32[]{:S(2)}, u32[]{:S(2)}) %collective-permute-start.6) | collective-permute-done | bytes 48 | tf_op jit(solution)/shard_map/ppermute | solution.py:34
  27.2 0.0 collective-permute-done.3.far_ref
  27.2 0.2 shard_map.107
  27.5 0.3 collective-permute-start.7
  27.8 0.5 collective-permute-start.8
  28.3 1.1 %collective-permute-start.9 = (bf16[2,16,512]{2,1,0:T(8,128)(2,1)S(1)}, bf16[2,16,512]{2,1,0:T(8,128)(2,1)S(1)}, u32[]{:S(2)}, u32[]{:S(2)}) collective-permute-start(bf16[2,16,512]{2,1,0:T(8,128)(2,1)S(1)} %get-tuple-element.48), channel_id=1, source_target_pairs={{0,24},{8,16},{16,8},{24,0},{1,25},{9,17},{17,9},{25,1},{2,26},{10... | collective-permute-start | bytes 98312 | tf_op jit(solution)/shard_map/ppermute | solution.py:34
  29.4 1.1 %shard_map.103 = (f32[4,8,1024]{2,1,0:T(8,128)S(1)}, f32[128,128]{1,0:T(8,128)S(1)}) custom-call(s32[1,128]{1,0:T(1,128)S(1)} %get-tuple-element.38.ids_ref, bf16[128,4096]{1,0:T(8,128)(2,1)S(1)} %get-tuple-element.36.q_ref.refs_0_.refs_2_, bf16[128,4096]{1,0:T(8,128)(2,1)S(1)} %get-tuple-element.37.g_ref.refs_1_.refs_3_, ...), custom_call_target="tpu_custom_call" | custom-call | flops 100000000 | bytes 100000 | tf_op jit(solution)/shard_map/pallas_call | solution.py:67
  30.4 0.0 collective-permute-done.kv_ref.refs_3_.refs_5_
  30.5 1.1 %shard_map.104 = (f32[4,8,1024]{2,1,0:T(8,128)S(1)}, f32[128,128]{1,0:T(8,128)S(1)}) custom-call(s32[1,128]{1,0:T(1,128)S(1)} %get-tuple-element.38.ids_ref, bf16[128,4096]{1,0:T(8,128)(2,1)S(1)} %get-tuple-element.36.q_ref.refs_0_.refs_2_, bf16[128,4096]{1,0:T(8,128)(2,1)S(1)} %get-tuple-element.37.g_ref.refs_1_.refs_3_, ...), custom_call_target="tpu_custom_call" | custom-call | flops 100000000 | bytes 100000 | tf_op jit(solution)/shard_map/pallas_call | solution.py:67
  31.6 0.0 collective-permute-done.7.refs_1_.refs_9_.refs_11_
  31.6 0.4 collective-permute-done.8.refs_2_.refs_10_.refs_12_
  32.0 0.0 collective-permute-done.9.refs_3_.refs_11_.refs_13_
  32.0 1.8 %shard_map.108 = (f32[4,8,1024]{2,1,0:T(8,128)S(1)}, bf16[2,16,512]{2,1,0:T(8,128)(2,1)S(1)}, bf16[2,16,512]{2,1,0:T(8,128)(2,1)S(1)}, bf16[2,16,512]{2,1,0:T(8,128)(2,1)S(1)}, bf16[2,16,512]{2,1,0:T(8,128)(2,1)S(1)}) custom-call(bf16[128,4096]{1,0:T(8,128)(2,1)S(1)} %get-tuple-element.36.q_ref.refs_0_.refs_2_, ...), custom_call_target="tpu_custom_call" | custom-call | flops 100000000 | bytes 100000 | tf_op jit(solution)/shard_map/pallas_call | solution.py:67
  33.7 0.2 collective-permute-start.11
  34.0 1.2 %collective-permute-start.12 = (bf16[2,16,512]{2,1,0:T(8,128)(2,1)S(1)}, bf16[2,16,512]{2,1,0:T(8,128)(2,1)S(1)}, u32[]{:S(2)}, u32[]{:S(2)}) collective-permute-start(bf16[2,16,512]{2,1,0:T(8,128)(2,1)S(1)} %get-tuple-element.60), channel_id=1, source_target_pairs={{0,16},{8,24},{16,0},{24,8},{1,17},{9,25},{17,1},{25,9},{2,18},{10... | collective-permute-start | bytes 98312 | tf_op jit(solution)/shard_map/ppermute | solution.py:34
  35.2 0.4 collective-permute-start.13
  35.7 1.6 %shard_map.111 = bf16[2,128,512]{2,1,0:T(8,128)(2,1)S(1)} custom-call(bf16[128,4096]{1,0:T(8,128)(2,1)S(1)} %get-tuple-element.36.q_ref.refs_0_.refs_2_, bf16[128,4096]{1,0:T(8,128)(2,1)S(1)} %get-tuple-element.37.g_ref.refs_1_.refs_3_, f32[4,8,1024]{2,1,0:T(8,128)S(1)} %get-tuple-element.49.refs_2_.refs_4_.final_ref, ...), custom_call_target="tpu_custom_call" | custom-call | flops 100000000 | bytes 100000 | tf_op jit(solution)/shard_map/pallas_call | solution.py:67
  37.3 2.0 %collective-permute-start.10 = (bf16[2,128,512]{2,1,0:T(8,128)(2,1)S(1)}, bf16[2,128,512]{2,1,0:T(8,128)(2,1)S(1)}, u32[]{:S(2)}, u32[]{:S(2)}) collective-permute-start(bf16[2,128,512]{2,1,0:T(8,128)(2,1)S(1)} %shard_map.111), channel_id=1, source_target_pairs={{0,7},{1,0},{2,1},{3,2},{4,3},{5,4},{6,5},{7,6},{8,15},{9,8},{10,9... | collective-permute-start | bytes 786440 | tf_op jit(solution)/shard_map/ppermute | solution.py:28
  39.3 0.0 collective-permute-done.11.refs_5_
  39.3 0.0 collective-permute-done.12.refs_6_
  39.3 0.0 collective-permute-done.13.refs_7_
  39.3 0.2 shard_map.113
  39.5 0.1 collective-permute-start.14
  39.7 9.1 %collective-permute-done.14.got_ref = bf16[4,2,16,512]{3,2,1,0:T(8,128)(2,1)S(1)} collective-permute-done((bf16[4,2,16,512]{3,2,1,0:T(8,128)(2,1)S(1)}, bf16[4,2,16,512]{3,2,1,0:T(8,128)(2,1)S(1)}, u32[]{:S(2)}, u32[]{:S(2)}) %collective-permute-start.14) | collective-permute-done | bytes 131104 | tf_op jit(solution)/shard_map/ppermute | solution.py:34
  48.8 0.1 collective-permute-start.15
  48.9 4.2 %collective-permute-done.15.got_ref = bf16[2,2,16,512]{3,2,1,0:T(8,128)(2,1)S(1)} collective-permute-done((bf16[2,2,16,512]{3,2,1,0:T(8,128)(2,1)S(1)}, bf16[2,2,16,512]{3,2,1,0:T(8,128)(2,1)S(1)}, u32[]{:S(2)}, u32[]{:S(2)}) %collective-permute-start.15) | collective-permute-done | bytes 65568 | tf_op jit(solution)/shard_map/ppermute | solution.py:34
  53.2 0.2 collective-permute-start.16
  53.4 2.7 %shard_map.109 = (bf16[128,4096]{1,0:T(8,128)(2,1)}, bf16[128,4096]{1,0:T(8,128)(2,1)}, f32[2,128,256]{2,1,0:T(8,128)S(1)}) custom-call(bf16[128,4096]{1,0:T(8,128)(2,1)S(1)} %get-tuple-element.36.q_ref.refs_0_.refs_2_, bf16[128,4096]{1,0:T(8,128)(2,1)S(1)} %get-tuple-element.37.g_ref.refs_1_.refs_3_, ...), custom_call_target="tpu_custom_call" | custom-call | flops 100000000 | bytes 100000 | tf_op jit(solution)/shard_map/pallas_call | solution.py:67
  56.1 2.7 %shard_map.110 = (bf16[128,4096]{1,0:T(8,128)(2,1)}, bf16[128,4096]{1,0:T(8,128)(2,1)}, f32[2,128,256]{2,1,0:T(8,128)S(1)}) custom-call(bf16[128,4096]{1,0:T(8,128)(2,1)} %get-tuple-element.52.refs_0_, bf16[128,4096]{1,0:T(8,128)(2,1)} %get-tuple-element.53.refs_1_, ...), custom_call_target="tpu_custom_call", output_to_operand_aliasing={{0}: (0, {}), {1}: (1, {})} | custom-call | flops 100000000 | bytes 100000 | tf_op jit(solution)/shard_map/pallas_call | solution.py:67
  58.8 0.0 collective-permute-done.10.next_ref
  58.8 0.2 shard_map.112
  59.0 0.8 %copy.16 = f32[1,128,2,512]{3,2,1,0:T(2,128)} copy(f32[1,128,2,512]{3,2,1,0:T(2,128)S(1)} %bitcast.11) | data formatting | bytes 1048576
  59.8 0.0 collective-permute-done.16.got_ref
  59.8 0.6 %copy.17 = f32[1,1,2,16,512]{4,3,2,1,0:T(8,128)} copy(f32[1,1,2,16,512]{4,3,2,1,0:T(8,128)S(1)} %bitcast.12) | data formatting | bytes 131072
  (5 shorter events, 0.1 us)
Async XLA Ops:
  1.6 4.7 %copy-start = (bf16[1,1,2,16,512]{4,3,2,1,0:T(8,128)(2,1)S(1)}, bf16[1,1,2,16,512]{4,3,2,1,0:T(8,128)(2,1)}, u32[]{:S(2)}) copy-start(bf16[1,1,2,16,512]{4,3,2,1,0:T(8,128)(2,1)} %param.10) | copy-start | bytes 98308
  3.3 27.1 %collective-permute-start = (bf16[144,1024]{1,0:T(8,128)(2,1)S(1)}, bf16[144,1024]{1,0:T(8,128)(2,1)S(1)}, u32[]{:S(2)}, u32[]{:S(2)}) collective-permute-start(bf16[144,1024]{1,0:T(8,128)(2,1)S(1)} %get-tuple-element.39.kv_ref.refs_4_.refs_6_), channel_id=1, source_target_pairs={{0,1},{1,2},{2,3},{3,4},{4,5},{5,6},{6,7},{7,0},{8,9},{9,10},{10,1... | collective-permute-start | bytes 884744 | tf_op jit(solution)/shard_map/ppermute | solution.py:28
  6.4 4.8 %collective-permute-start.1 = (bf16[1,2,16,512]{3,2,1,0:T(8,128)(2,1)S(1)}, bf16[1,2,16,512]{3,2,1,0:T(8,128)(2,1)S(1)}, u32[]{:S(2)}, u32[]{:S(2)}) collective-permute-start(bf16[1,2,16,512]{3,2,1,0:T(8,128)(2,1)S(1)} %bitcast.20), channel_id=1, source_target_pairs={{0,4},{1,5},{2,6},{3,7},{4,0},{5,1},{6,2},{7,3},{8,12},{9,13},{10,... | collective-permute-start | bytes 98312 | tf_op jit(solution)/shard_map/ppermute | solution.py:34
  11.2 4.3 %collective-permute-start.2 = (bf16[2,2,16,512]{3,2,1,0:T(8,128)(2,1)S(1)}, bf16[2,2,16,512]{3,2,1,0:T(8,128)(2,1)S(1)}, u32[]{:S(2)}, u32[]{:S(2)}) collective-permute-start(bf16[2,2,16,512]{3,2,1,0:T(8,128)(2,1)S(1)} %shard_map.105.a_ref), channel_id=1, source_target_pairs={{0,2},{1,3},{2,0},{3,1},{4,6},{5,7},{6,4},{7,5},{8,10},{9,11},{10,... | collective-permute-start | bytes 196616 | tf_op jit(solution)/shard_map/ppermute | solution.py:34
  15.5 11.8 %collective-permute-start.3 = (bf16[4,2,16,512]{3,2,1,0:T(8,128)(2,1)S(1)}, bf16[4,2,16,512]{3,2,1,0:T(8,128)(2,1)S(1)}, u32[]{:S(2)}, u32[]{:S(2)}) collective-permute-start(bf16[4,2,16,512]{3,2,1,0:T(8,128)(2,1)S(1)} %shard_map.106.near_ref), channel_id=1, source_target_pairs={{0,1},{1,0},{2,3},{3,2},{4,5},{5,4},{6,7},{7,6},{8,9},{9,8},{10,11... | collective-permute-start | bytes 393224 | tf_op jit(solution)/shard_map/ppermute | solution.py:34
  22.7 1.9 %collective-permute-start.4 = (s32[1,4]{1,0:T(1,128)S(1)}, s32[1,4]{1,0:T(1,128)S(1)}, u32[]{:S(2)}, u32[]{:S(2)}) collective-permute-start(s32[1,4]{1,0:T(1,128)S(1)} %get-tuple-element.44.refs_0_), channel_id=1, source_target_pairs={{0,8},{8,0},{16,24},{24,16},{1,9},{9,1},{17,25},{25,17},{2,10},{10... | collective-permute-start | bytes 56 | tf_op jit(solution)/shard_map/ppermute | solution.py:34
  22.7 3.6 %collective-permute-start.5 = (s32[1,4]{1,0:T(1,128)S(1)}, s32[1,4]{1,0:T(1,128)S(1)}, u32[]{:S(2)}, u32[]{:S(2)}) collective-permute-start(s32[1,4]{1,0:T(1,128)S(1)} %get-tuple-element.44.refs_0_), channel_id=1, source_target_pairs={{0,16},{8,24},{16,0},{24,8},{1,17},{9,25},{17,1},{25,9},{2,18},{10... | collective-permute-start | bytes 56 | tf_op jit(solution)/shard_map/ppermute | solution.py:34
  24.2 3.0 %collective-permute-start.6 = (s32[1,4]{1,0:T(1,128)S(1)}, s32[1,4]{1,0:T(1,128)S(1)}, u32[]{:S(2)}, u32[]{:S(2)}) collective-permute-start(s32[1,4]{1,0:T(1,128)S(1)} %get-tuple-element.44.refs_0_), channel_id=1, source_target_pairs={{0,24},{8,16},{16,8},{24,0},{1,25},{9,17},{17,9},{25,1},{2,26},{10... | collective-permute-start | bytes 56 | tf_op jit(solution)/shard_map/ppermute | solution.py:34
  27.5 4.1 %collective-permute-start.7 = (bf16[2,16,512]{2,1,0:T(8,128)(2,1)S(1)}, bf16[2,16,512]{2,1,0:T(8,128)(2,1)S(1)}, u32[]{:S(2)}, u32[]{:S(2)}) collective-permute-start(bf16[2,16,512]{2,1,0:T(8,128)(2,1)S(1)} %get-tuple-element.46), channel_id=1, source_target_pairs={{0,8},{8,0},{16,24},{24,16},{1,9},{9,1},{17,25},{25,17},{2,10},{10... | collective-permute-start | bytes 98312 | tf_op jit(solution)/shard_map/ppermute | solution.py:34
  27.8 4.2 %collective-permute-start.8 = (bf16[2,16,512]{2,1,0:T(8,128)(2,1)S(1)}, bf16[2,16,512]{2,1,0:T(8,128)(2,1)S(1)}, u32[]{:S(2)}, u32[]{:S(2)}) collective-permute-start(bf16[2,16,512]{2,1,0:T(8,128)(2,1)S(1)} %get-tuple-element.47), channel_id=1, source_target_pairs={{0,16},{8,24},{16,0},{24,8},{1,17},{9,25},{17,1},{25,9},{2,18},{10... | collective-permute-start | bytes 98312 | tf_op jit(solution)/shard_map/ppermute | solution.py:34
  28.3 3.7 %collective-permute-start.9 = (bf16[2,16,512]{2,1,0:T(8,128)(2,1)S(1)}, bf16[2,16,512]{2,1,0:T(8,128)(2,1)S(1)}, u32[]{:S(2)}, u32[]{:S(2)}) collective-permute-start(bf16[2,16,512]{2,1,0:T(8,128)(2,1)S(1)} %get-tuple-element.48), channel_id=1, source_target_pairs={{0,24},{8,16},{16,8},{24,0},{1,25},{9,17},{17,9},{25,1},{2,26},{10... | collective-permute-start | bytes 98312 | tf_op jit(solution)/shard_map/ppermute | solution.py:34
  33.7 5.5 %collective-permute-start.11 = (bf16[2,16,512]{2,1,0:T(8,128)(2,1)S(1)}, bf16[2,16,512]{2,1,0:T(8,128)(2,1)S(1)}, u32[]{:S(2)}, u32[]{:S(2)}) collective-permute-start(bf16[2,16,512]{2,1,0:T(8,128)(2,1)S(1)} %get-tuple-element.59), channel_id=1, source_target_pairs={{0,8},{8,0},{16,24},{24,16},{1,9},{9,1},{17,25},{25,17},{2,10},{10... | collective-permute-start | bytes 98312 | tf_op jit(solution)/shard_map/ppermute | solution.py:34
  34.0 5.3 %collective-permute-start.12 = (bf16[2,16,512]{2,1,0:T(8,128)(2,1)S(1)}, bf16[2,16,512]{2,1,0:T(8,128)(2,1)S(1)}, u32[]{:S(2)}, u32[]{:S(2)}) collective-permute-start(bf16[2,16,512]{2,1,0:T(8,128)(2,1)S(1)} %get-tuple-element.60), channel_id=1, source_target_pairs={{0,16},{8,24},{16,0},{24,8},{1,17},{9,25},{17,1},{25,9},{2,18},{10... | collective-permute-start | bytes 98312 | tf_op jit(solution)/shard_map/ppermute | solution.py:34
  35.2 4.1 %collective-permute-start.13 = (bf16[2,16,512]{2,1,0:T(8,128)(2,1)S(1)}, bf16[2,16,512]{2,1,0:T(8,128)(2,1)S(1)}, u32[]{:S(2)}, u32[]{:S(2)}) collective-permute-start(bf16[2,16,512]{2,1,0:T(8,128)(2,1)S(1)} %get-tuple-element.61), channel_id=1, source_target_pairs={{0,24},{8,16},{16,8},{24,0},{1,25},{9,17},{17,9},{25,1},{2,26},{10... | collective-permute-start | bytes 98312 | tf_op jit(solution)/shard_map/ppermute | solution.py:34
  37.3 21.5 %collective-permute-start.10 = (bf16[2,128,512]{2,1,0:T(8,128)(2,1)S(1)}, bf16[2,128,512]{2,1,0:T(8,128)(2,1)S(1)}, u32[]{:S(2)}, u32[]{:S(2)}) collective-permute-start(bf16[2,128,512]{2,1,0:T(8,128)(2,1)S(1)} %shard_map.111), channel_id=1, source_target_pairs={{0,7},{1,0},{2,1},{3,2},{4,3},{5,4},{6,5},{7,6},{8,15},{9,8},{10,9... | collective-permute-start | bytes 786440 | tf_op jit(solution)/shard_map/ppermute | solution.py:28
  39.5 9.3 %collective-permute-start.14 = (bf16[4,2,16,512]{3,2,1,0:T(8,128)(2,1)S(1)}, bf16[4,2,16,512]{3,2,1,0:T(8,128)(2,1)S(1)}, u32[]{:S(2)}, u32[]{:S(2)}) collective-permute-start(bf16[4,2,16,512]{3,2,1,0:T(8,128)(2,1)S(1)} %get-tuple-element.63), channel_id=1, source_target_pairs={{0,1},{1,0},{2,3},{3,2},{4,5},{5,4},{6,7},{7,6},{8,9},{9,8},{10,11... | collective-permute-start | bytes 393224 | tf_op jit(solution)/shard_map/ppermute | solution.py:34
  48.8 4.3 %collective-permute-start.15 = (bf16[2,2,16,512]{3,2,1,0:T(8,128)(2,1)S(1)}, bf16[2,2,16,512]{3,2,1,0:T(8,128)(2,1)S(1)}, u32[]{:S(2)}, u32[]{:S(2)}) collective-permute-start(bf16[2,2,16,512]{3,2,1,0:T(8,128)(2,1)S(1)} %get-tuple-element.65), channel_id=1, source_target_pairs={{0,2},{1,3},{2,0},{3,1},{4,6},{5,7},{6,4},{7,5},{8,10},{9,11},{10,... | collective-permute-start | bytes 196616 | tf_op jit(solution)/shard_map/ppermute | solution.py:34
  53.2 6.6 %collective-permute-start.16 = (bf16[1,2,16,512]{3,2,1,0:T(8,128)(2,1)S(1)}, bf16[1,2,16,512]{3,2,1,0:T(8,128)(2,1)S(1)}, u32[]{:S(2)}, u32[]{:S(2)}) collective-permute-start(bf16[1,2,16,512]{3,2,1,0:T(8,128)(2,1)S(1)} %get-tuple-element.67), channel_id=1, source_target_pairs={{0,4},{1,5},{2,6},{3,7},{4,0},{5,1},{6,2},{7,3},{8,12},{9,13},{10,... | collective-permute-start | bytes 98312 | tf_op jit(solution)/shard_map/ppermute | solution.py:34

commit v3 on v2

--- a/solution.py
+++ b/solution.py
@@ -18,14 +18,18 @@
 BF = jnp.bfloat16
 F32 = jnp.float32
 PACK = 16
-GATHER_FIRST = []
-SCATTER_FIRST = [1]
+CHAIN_F = True
+CHAIN_R = True
+REST_BOUNDS = [2]
 VMEM_LIMIT = 24 * 1024 * 1024
 
 
-def ring(block, axis, distance):
+def ring(block, axis, distance, chain):
     size = lax.axis_size(axis)
-    return lax.ppermute(block, axis, [(i, (i + distance) % size) for i in range(size)])
+    route = [(i, (i + distance) % size) for i in range(size)]
+    if chain:
+        route = [(i, j) for i, j in route if j == i + distance]
+    return lax.ppermute(block, axis, route)
 
 
 def swap(block, axis, k):
@@ -76,34 +80,54 @@
     )(*args)
 
 
-def join_kernel(a_ref, b_ref, out_ref):
-    count = a_ref.shape[0]
-    out_ref[:count] = a_ref[...]
-    out_ref[count:] = b_ref[...]
-
-
-def prepare_kernel(
-    ids_hbm, reach_hbm, owners_hbm, q_hbm, g_hbm, seg_hbm, kv_ref,
-    ids_ref, owners_ref, q_ref, g_ref, seg_ref, payload_ref, tbias_ref, reach_ref, sems,
+def join_kernel(*refs):
+    for i, ref in enumerate(refs[:-1]):
+        refs[-1][i] = ref[0]
+
+
+def pack_kernel(
+    ids_hbm, owners_hbm, seg_hbm, kv_ref, ids_ref, owners_ref, seg_ref, payload_ref, sems
 ):
-    copies = [
-        pltpu.make_async_copy(src, dst, sems.at[i])
-        for i, (src, dst) in enumerate(
-            (
-                (ids_hbm, ids_ref), (reach_hbm, reach_ref), (owners_hbm, owners_ref),
-                (seg_hbm, seg_ref), (q_hbm, q_ref), (g_hbm, g_ref),
-            )
-        )
-    ]
+    pairs = ((ids_hbm, ids_ref), (owners_hbm, owners_ref), (seg_hbm, seg_ref))
+    copies = [pltpu.make_async_copy(src, dst, sems.at[i]) for i, (src, dst) in enumerate(pairs)]
     for copy in copies:
         copy.start()
     n = kv_ref.shape[0]
     payload_ref[:n] = kv_ref[...]
     payload_ref[n:] = jnp.zeros((PACK, kv_ref.shape[1]), BF)
-    copies[0].wait()
-    copies[1].wait()
+    for copy in copies:
+        copy.wait()
+    tags = jnp.broadcast_to((ids_ref[...] + 1).astype(F32), (PACK, n))
+    payload_ref[n:, 0:n] = tags.astype(BF)
+
+
+def scored(keys, values, q_rows, g_rows, bias):
+    return dot(keys, q_rows, 1, 1) * (SCALE * LOG2E) + bias, dot(values, g_rows, 1, 1)
+
+
+def own_kernel(
+    reach_hbm, q_hbm, g_hbm, ids_ref, kv_ref,
+    q_ref, g_ref, stats_ref, bias_ref, tbias_ref, reach_ref, sems,
+):
+    n = q_ref.shape[0]
+    heads = stats_ref.shape[0]
+    part = GROUP * DH
+    first = pltpu.make_async_copy(reach_hbm, reach_ref, sems.at[2, 0])
+    first.start()
+    copies = []
+    for h in range(heads):
+        some = pl.ds(h * part, part)
+        for i, (src, dst) in enumerate(((q_hbm, q_ref), (g_hbm, g_ref))):
+            copy = pltpu.make_async_copy(src.at[:, some], dst.at[:, some], sems.at[i, h])
+            copy.start()
+            copies.append(copy)
     ids = ids_ref[...]
-    payload_ref[n:, 0:n] = jnp.broadcast_to((ids + 1).astype(F32), (PACK, n)).astype(BF)
+    id_cols = jnp.broadcast_to(ids.astype(F32), (n, n))
+    k_idx = lax.broadcasted_iota(jnp.int32, (n, n), 0)
+    q_idx = lax.broadcasted_iota(jnp.int32, (n, n), 1)
+    bias_ref[...] = as_bias((id_cols.T == id_cols) & (k_idx <= q_idx))
+    bias = tile_heads(bias_ref[...])
+    first.wait()
     reach_row = jnp.zeros((1, n), jnp.int32)
     for b in range(reach_ref.shape[1]):
         reach_row = jnp.where(ids == b, reach_ref[0:1, b : b + 1], reach_row)
@@ -113,23 +137,9 @@
     for k in range(depths):
         row = as_bias((me ^ k) < reach_row)
         tbias_ref[k * seg_len : (k + 1) * seg_len] = jnp.broadcast_to(row, (seg_len, n))
-    for copy in copies[2:]:
-        copy.wait()
-
-
-def scored(keys, values, q_rows, g_rows, bias):
-    return dot(keys, q_rows, 1, 1) * (SCALE * LOG2E) + bias, dot(values, g_rows, 1, 1)
-
-
-def own_kernel(ids_ref, q_ref, g_ref, kv_ref, stats_ref, bias_ref):
-    n = q_ref.shape[0]
-    heads = stats_ref.shape[0]
-    id_cols = jnp.broadcast_to(ids_ref[...].astype(F32), (n, n))
-    k_idx = lax.broadcasted_iota(jnp.int32, (n, n), 0)
-    q_idx = lax.broadcasted_iota(jnp.int32, (n, n), 1)
-    bias_ref[...] = as_bias((id_cols.T == id_cols) & (k_idx <= q_idx))
-    bias = tile_heads(bias_ref[...])
     for h in range(heads):
+        copies[2 * h].wait()
+        copies[2 * h + 1].wait()
         scores, grad_w = scored(
             kv_ref[:n, cols(h)], kv_ref[:n, cols(h + heads)],
             head_rows(q_ref, h), head_rows(g_ref, h), bias,
@@ -227,7 +237,7 @@
     heads = final_ref.shape[0]
     part = GROUP * DH
     bias = tile_heads(jnp.concatenate([obias_ref[...], ebias_ref[...], tbias_ref[...]], axis=0))
-    copies = []
+    copies, late = [], []
     for i, h in enumerate(some):
         keys = jnp.concatenate(
             [kv_ref[:n, cols(h)], ekv_ref[:n, cols(h)]] + [s[0, :, cols(h)] for s in seg_refs],
@@ -254,8 +264,10 @@
             )
             copy.start()
             copies.append(copy)
-        dkv_ref[0, :, cols(i)] = dot(score_grad[:n], q_rows, 1, 0) * SCALE
-        dkv_ref[1, :, cols(i)] = dot(weights_bf[:n], g_rows, 1, 0)
+        late.append((i, score_grad[:n], q_rows, weights_bf[:n], g_rows))
+    for i, score_grad, q_rows, weights_bf, g_rows in late:
+        dkv_ref[0, :, cols(i)] = dot(score_grad, q_rows, 1, 0) * SCALE
+        dkv_ref[1, :, cols(i)] = dot(weights_bf, g_rows, 1, 0)
     for copy in copies:
         copy.wait()
 
@@ -298,10 +310,16 @@
                 out_ref[i, which] = total.astype(out_ref.dtype)
 
 
-def fold_kernel(kept_ref, got_ref, *out_refs, places):
-    for out_ref, where in zip(out_refs, places):
-        for i, p in enumerate(where):
-            out_ref[i] = (kept_ref[p] + got_ref[p].astype(F32)).astype(out_ref.dtype)
+def fold_kernel(kept_ref, got_ref, *out_refs):
+    for i, out_ref in enumerate(out_refs):
+        out_ref[0] = (kept_ref[i] + got_ref[i].astype(F32)).astype(out_ref.dtype)
+
+
+def last_kernel(total_ref, *refs):
+    total = total_ref[...]
+    for ref in refs[:-1]:
+        total = total + ref[...].astype(F32)
+    refs[-1][...] = total
 
 
 def combine_kernel(next_ref, *refs):
@@ -326,31 +344,38 @@
     tbias_shape = ((depths * seg_len, n), F32)
     assert branch_reach.shape[1] < 256 and n_branch & (n_branch - 1) == 0
 
-    bits = [1 << i for i in range(n_branch.bit_length() - 1)][::-1]
-    bits = GATHER_FIRST + [x for x in bits if x not in GATHER_FIRST]
-    offsets, bit = [0], bits[0]
-    far = swap(trunk_kv[0], "branch", bit)
-    offsets = offsets + [bit ^ o for o in offsets]
+    steps = list(range(2, n_branch, 2))
+    offsets = [0] + steps
+    offsets = offsets + [1 ^ o for o in offsets]
+    pieces = []
+    for k in steps:
+        pieces.append(swap(trunk_kv[0], "branch", k))
     own_kv = keys_values[0].reshape(n, 2 * kv_width)
-    ids, own_owners, q, g, near, payload, tbias = call(
-        prepare_kernel,
+    ids, own_owners, own_seg, payload = call(
+        pack_kernel,
         [
-            ((1, n), jnp.int32), ((1, depths), jnp.int32), ((n, width), BF), ((n, width), BF),
-            ((1,) + seg_shape, BF), ((n + PACK, 2 * kv_width), BF), tbias_shape,
+            ((1, n), jnp.int32), ((1, depths), jnp.int32),
+            ((1,) + seg_shape, BF), ((n + PACK, 2 * kv_width), BF),
         ],
-        branch_of, branch_reach, ancestors[0], queries[0], out_grad[0], trunk_kv[0], own_kv,
-        hbm=6,
-        scratch=[pltpu.VMEM(branch_reach.shape, jnp.int32), pltpu.SemaphoreType.DMA((6,))],
-    )
-    earlier = ring(payload, "branch", 1)
+        branch_of, ancestors[0], trunk_kv[0], own_kv,
+        hbm=3,
+        scratch=[pltpu.SemaphoreType.DMA((3,))],
+    )
+    earlier = ring(payload, "branch", 1, CHAIN_F)
     owners = [own_owners]
     for k in range(1, depths):
-        owners.append(swap(own_owners, "trunk", k))
-    for step, bit in enumerate(bits[1:], 1):
-        (near,) = call(join_kernel, [((2 * near.shape[0],) + seg_shape, BF)], near, far)
-        far = swap(near, "branch", bit)
-        offsets = offsets + [bit ^ o for o in offsets]
-    stats0, obias = call(own_kernel, [stats_shape, bias_shape], ids, q, g, payload)
+        owners.append(swap(ancestors[0], "trunk", k))
+    (near,) = call(join_kernel, [((n_branch // 2,) + seg_shape, BF)], own_seg, *pieces)
+    far = swap(near, "branch", 1)
+    q, g, stats0, obias, tbias = call(
+        own_kernel,
+        [((n, width), BF), ((n, width), BF), stats_shape, bias_shape, tbias_shape],
+        branch_reach, queries[0], out_grad[0], ids, payload,
+        hbm=3,
+        scratch=[
+            pltpu.VMEM(branch_reach.shape, jnp.int32), pltpu.SemaphoreType.DMA((3, heads)),
+        ],
+    )
     stats1, ebias = call(earlier_kernel, [stats_shape, bias_shape], ids, q, g, earlier, stats0)
     picked = call(
         functools.partial(pick_kernel, offsets=offsets), [(seg_shape, BF)] * depths,
@@ -370,36 +395,23 @@
         earlier_grad_kernel, [((2, n, kv_width), BF)],
         q, g, final, earlier, ebias,
     )
-    from_next = ring(earlier_part, "branch", -1)
-    keeps = list(range(n_branch))
-    order = [1 << i for i in range(n_branch.bit_length() - 1)]
-    order = SCATTER_FIRST + [x for x in order if x not in SCATTER_FIRST]
-    order = [x for x in order if x < n_branch]
-    for step, bit in enumerate(order):
-        places = [[i for i, o in enumerate(keeps) if not o & bit]]
-        places += [[i for i, o in enumerate(keeps) if o & bit]]
-        sends = [keeps[i] for i in places[1]]
-        keeps = [keeps[i] for i in places[0]]
-        sends = [o ^ bit for o in sends]
-        assert sends == keeps
-        half = (len(keeps),) + seg_shape
-        outs = [(half, BF), (half, F32)]
-        if step == 0:
-            send, kept = call(
-                functools.partial(split_kernel, keeps=keeps, sends=[o ^ bit for o in keeps]),
-                outs, *owners, *returned,
-            )
-        else:
-            send, kept = call(functools.partial(fold_kernel, places=places[::-1]), outs, kept, got)
-        got = swap(send, "branch", bit)
-    (trunk_grad,) = call(
-        functools.partial(fold_kernel, places=[[0]]),
-        [((1,) + seg_shape, F32)], kept, got,
-    )
+    from_next = ring(earlier_part, "branch", -1, CHAIN_R)
+    half, one = (n_branch // 2,) + seg_shape, (1,) + seg_shape
+    keeps = [0] + steps
+    send, kept = call(
+        functools.partial(split_kernel, keeps=keeps, sends=[o ^ 1 for o in keeps]),
+        [(half, BF), (half, F32)], *owners, *returned,
+    )
+    got = swap(send, "branch", 1)
+    total, *sends = call(fold_kernel, [(one, F32)] + [(one, BF)] * len(steps), kept, got)
+    pieces = []
+    for k, send in zip(steps, sends):
+        pieces.append(swap(send, "branch", k))
+    (trunk_grad,) = call(last_kernel, [(one, F32)], total, *pieces)
     own_parts, outputs = [], []
-    halves = 2
-    for part in range(halves):
-        some = list(range(heads))[part * heads // halves : (part + 1) * heads // halves]
+    bounds = [0] + [min(x, heads) for x in REST_BOUNDS] + [heads]
+    for part, (first, end) in enumerate(zip(bounds[:-1], bounds[1:])):
+        some = list(range(first, end))
         *outputs, own_part = call(
             functools.partial(rest_kernel, some=some, aliased=part > 0),
             [((n, width), BF), ((n, width), BF), ((2, n, len(some) * DH), F32)],

time: 60.6 us -> 58.1 us (0.959)
  waiting for transfers between devices: 21.3 us -> 16.2 us
  starting transfers between devices: 22.6 us -> 23.9 us
    ppermute x15 -> x17, waiting for transfers between devices: 21.3 us -> 16.2 us  [swap(): lax.ppermute(block, axis, [(i, i ^ k) for i in range(lax.axis_size(axis))])]
    ppermute x2, starting transfers between devices: 5.05 us -> 6.21 us  [ring(): return lax.ppermute(block, axis, route)]
    pallas_call x15 -> x13, Pallas kernels: 13.3 us -> 13.9 us  [call(): pl.pallas_call(kernel, in_specs=[hspec] * hbm + [vspec] * (len(args) - hb...]
    unnamed x5 -> x7, local copies, waits for them, and re-layouts: 2.41 us -> 2.97 us
    ppermute x15 -> x17, starting transfers between devices: 17.6 us -> 17.7 us  [swap(): lax.ppermute(block, axis, [(i, i ^ k) for i in range(lax.axis_size(axis))])]
  transfers between devices with their start and end apart: 17 -> 19, of which waited for: 7 -> 8; matrix products, arithmetic and copies ran while one was open for 1% -> 1% of each run, Pallas kernels for 16% -> 17%
where the time goes in v3:
time: 58.1 us; the launch traced here: 57.8 us
  starting transfers between devices  23.9 us (41%)
  waiting for transfers between devices  16.2 us (28%)
  Pallas kernels  13.9 us (24%)
  local copies, waits for them, and re-layouts  2.97 us (5%)
  between operations  0.81 us (1%)
    ppermute x17, starting transfers between devices, swap(): lax.ppermute(block, axis, [(i, i ^ k) for i in range(lax.axis_size(axis))])  17.7 us
    ppermute x17, waiting for transfers between devices, swap(): lax.ppermute(block, axis, [(i, i ^ k) for i in range(lax.axis_size(axis))])  16.2 us
    pallas_call x13, Pallas kernels, call(): pl.pallas_call(kernel, in_specs=[hspec] * hbm + [vspec] * (len(args) - hb...  13.9 us
    ppermute x2, starting transfers between devices, ring(): return lax.ppermute(block, axis, route)  6.21 us
    unnamed x7, local copies, waits for them, and re-layouts  2.97 us
  transfers between devices with their start and end apart: 19, of which 8 were waited for; matrix products, arithmetic and copies ran while one was open for 1% of the time, Pallas kernels for 17%

profile of v3, /device:TPU:0, one launch (start us, length us, event | category | flops | bytes accessed | tf_op | source)
XLA Modules:
  0.0 57.8 jit_solution(1202461211802117856)
XLA Ops:
  0.6 1.0 %copy.13 = bf16[16,8,2,512]{3,1,2,0:T(8,128)(2,1)S(1)} copy(bf16[16,8,2,512]{3,2,1,0:T(2,128)(2,1)} %bitcast.18) | data formatting | bytes 524288
  1.6 0.0 copy-start
  1.6 0.9 %shard_map.102 = (s32[1,128]{1,0:T(1,128)S(1)}, s32[1,4]{1,0:T(1,128)S(1)}, bf16[1,2,16,512]{3,2,1,0:T(8,128)(2,1)S(1)}, bf16[144,1024]{1,0:T(8,128)(2,1)S(1)}) custom-call(s32[1,128]{1,0:T(1,128)} %ids_hbm.1, s32[1,4]{1,0:T(1,128)} %bitcast.23, bf16[1,2,16,512]{3,2,1,0:T(8,128)(2,1)} %bitcast.19, bf16[128,1024]{1,0:T(8,128)(2,1)S(1)} %bitcast.13), custom_call_target="tpu_custom_call" | custom-call | flops 100000000 | bytes 100000 | tf_op jit(solution)/shard_map/pallas_call | solution.py:71
  2.5 4.9 %collective-permute-start = (bf16[144,1024]{1,0:T(8,128)(2,1)S(1)}, bf16[144,1024]{1,0:T(8,128)(2,1)S(1)}, u32[]{:S(2)}, u32[]{:S(2)}) collective-permute-start(bf16[144,1024]{1,0:T(8,128)(2,1)S(1)} %get-tuple-element.37.kv_ref.refs_4_.refs_6_), channel_id=1, source_target_pairs={{0,1},{1,2},{2,3},{3,4},{4,5},{5,6},{6,7},{8,9},{9,10},{10,11},{11... | collective-permute-start | bytes 884744 | tf_op jit(solution)/shard_map/ppermute | solution.py:32
  7.4 0.0 copy-done
  7.4 1.6 %collective-permute-start.1 = (bf16[1,2,16,512]{3,2,1,0:T(8,128)(2,1)S(1)}, bf16[1,2,16,512]{3,2,1,0:T(8,128)(2,1)S(1)}, u32[]{:S(2)}, u32[]{:S(2)}) collective-permute-start(bf16[1,2,16,512]{3,2,1,0:T(8,128)(2,1)S(1)} %bitcast.20), channel_id=1, source_target_pairs={{0,2},{1,3},{2,0},{3,1},{4,6},{5,7},{6,4},{7,5},{8,10},{9,11},{10,... | collective-permute-start | bytes 98312 | tf_op jit(solution)/shard_map/ppermute | solution.py:38
  9.1 2.6 %collective-permute-start.2 = (bf16[1,2,16,512]{3,2,1,0:T(8,128)(2,1)S(1)}, bf16[1,2,16,512]{3,2,1,0:T(8,128)(2,1)S(1)}, u32[]{:S(2)}, u32[]{:S(2)}) collective-permute-start(bf16[1,2,16,512]{3,2,1,0:T(8,128)(2,1)S(1)} %bitcast.21), channel_id=1, source_target_pairs={{0,4},{1,5},{2,6},{3,7},{4,0},{5,1},{6,2},{7,3},{8,12},{9,13},{10,... | collective-permute-start | bytes 98312 | tf_op jit(solution)/shard_map/ppermute | solution.py:38
  11.6 0.2 collective-permute-start.3
  11.9 0.0 collective-permute-done.1.refs_1_
  11.9 2.3 %collective-permute-done.2.refs_2_ = bf16[1,2,16,512]{3,2,1,0:T(8,128)(2,1)S(1)} collective-permute-done((bf16[1,2,16,512]{3,2,1,0:T(8,128)(2,1)S(1)}, bf16[1,2,16,512]{3,2,1,0:T(8,128)(2,1)S(1)}, u32[]{:S(2)}, u32[]{:S(2)}) %collective-permute-start.2) | collective-permute-done | bytes 32800 | tf_op jit(solution)/shard_map/ppermute | solution.py:38
  14.2 3.2 %collective-permute-done.3.refs_3_ = bf16[1,2,16,512]{3,2,1,0:T(8,128)(2,1)S(1)} collective-permute-done((bf16[1,2,16,512]{3,2,1,0:T(8,128)(2,1)S(1)}, bf16[1,2,16,512]{3,2,1,0:T(8,128)(2,1)S(1)}, u32[]{:S(2)}, u32[]{:S(2)}) %collective-permute-start.3) | collective-permute-done | bytes 32800 | tf_op jit(solution)/shard_map/ppermute | solution.py:38
  17.4 0.0 copy-start.1
  17.4 0.1 collective-permute-start.4
  17.5 0.6 copy-done.1
  18.0 0.0 collective-permute-start.5
  18.0 1.5 %collective-permute-start.6 = (s32[1,4]{1,0:T(1,128)S(1)}, s32[1,4]{1,0:T(1,128)S(1)}, u32[]{:S(2)}, u32[]{:S(2)}) collective-permute-start(s32[1,4]{1,0:T(1,128)S(1)} %bitcast.25), channel_id=1, source_target_pairs={{0,16},{8,24},{16,0},{24,8},{1,17},{9,25},{17,1},{25,9},{2,18},{10... | collective-permute-start | bytes 56 | tf_op jit(solution)/shard_map/ppermute | solution.py:38
  19.5 0.4 collective-permute-start.7
  19.9 0.0 collective-permute-done.5.refs_1_
  19.9 1.7 %collective-permute-done.6.refs_2_ = s32[1,4]{1,0:T(1,128)S(1)} collective-permute-done((s32[1,4]{1,0:T(1,128)S(1)}, s32[1,4]{1,0:T(1,128)S(1)}, u32[]{:S(2)}, u32[]{:S(2)}) %collective-permute-start.6) | collective-permute-done | bytes 48 | tf_op jit(solution)/shard_map/ppermute | solution.py:38
  21.6 0.9 %collective-permute-done.7.refs_3_ = s32[1,4]{1,0:T(1,128)S(1)} collective-permute-done((s32[1,4]{1,0:T(1,128)S(1)}, s32[1,4]{1,0:T(1,128)S(1)}, u32[]{:S(2)}, u32[]{:S(2)}) %collective-permute-start.7) | collective-permute-done | bytes 48 | tf_op jit(solution)/shard_map/ppermute | solution.py:38
  22.5 0.0 collective-permute-done.4.far_ref
  22.5 0.2 shard_map.106
  22.8 0.3 collective-permute-start.8
  23.0 1.2 %collective-permute-start.9 = (bf16[2,16,512]{2,1,0:T(8,128)(2,1)S(1)}, bf16[2,16,512]{2,1,0:T(8,128)(2,1)S(1)}, u32[]{:S(2)}, u32[]{:S(2)}) collective-permute-start(bf16[2,16,512]{2,1,0:T(8,128)(2,1)S(1)} %get-tuple-element.47), channel_id=1, source_target_pairs={{0,16},{8,24},{16,0},{24,8},{1,17},{9,25},{17,1},{25,9},{2,18},{10... | collective-permute-start | bytes 98312 | tf_op jit(solution)/shard_map/ppermute | solution.py:38
  24.3 0.4 collective-permute-start.10
  24.7 2.5 %shard_map.103 = (bf16[128,4096]{1,0:T(8,128)(2,1)S(1)}, bf16[128,4096]{1,0:T(8,128)(2,1)S(1)}, f32[4,8,1024]{2,1,0:T(8,128)S(1)}, f32[128,128]{1,0:T(8,128)S(1)}, f32[64,128]{1,0:T(8,128)S(1)}) custom-call(s32[1,16]{1,0:T(1,128)} %reach_hbm.1, bf16[128,4096]{1,0:T(8,128)(2,1)} %bitcast.16, bf16[128,4096]{1,0:T(8,128)(2,1)} %bitcast.17, ...), custom_call_target="tpu_custom_call" | custom-call | flops 100000000 | bytes 100000 | tf_op jit(solution)/shard_map/pallas_call | solution.py:71
  27.2 0.0 collective-permute-done.kv_ref.refs_3_.refs_5_
  27.2 1.1 %shard_map.104 = (f32[4,8,1024]{2,1,0:T(8,128)S(1)}, f32[128,128]{1,0:T(8,128)S(1)}) custom-call(s32[1,128]{1,0:T(1,128)S(1)} %get-tuple-element.36.ids_ref, bf16[128,4096]{1,0:T(8,128)(2,1)S(1)} %get-tuple-element.38.q_ref.refs_0_.refs_2_, bf16[128,4096]{1,0:T(8,128)(2,1)S(1)} %get-tuple-element.39.g_ref.refs_1_.refs_3_, ...), custom_call_target="tpu_custom_call" | custom-call | flops 100000000 | bytes 100000 | tf_op jit(solution)/shard_map/pallas_call | solution.py:71
  28.4 0.0 collective-permute-done.8.refs_1_.refs_9_.refs_11_
  28.4 0.0 collective-permute-done.9.refs_2_.refs_10_.refs_12_
  28.4 0.0 collective-permute-done.10.refs_3_.refs_11_.refs_13_
  28.4 1.8 %shard_map.107 = (f32[4,8,1024]{2,1,0:T(8,128)S(1)}, bf16[2,16,512]{2,1,0:T(8,128)(2,1)S(1)}, bf16[2,16,512]{2,1,0:T(8,128)(2,1)S(1)}, bf16[2,16,512]{2,1,0:T(8,128)(2,1)S(1)}, bf16[2,16,512]{2,1,0:T(8,128)(2,1)S(1)}) custom-call(bf16[128,4096]{1,0:T(8,128)(2,1)S(1)} %get-tuple-element.38.q_ref.refs_0_.refs_2_, ...), custom_call_target="tpu_custom_call" | custom-call | flops 100000000 | bytes 100000 | tf_op jit(solution)/shard_map/pallas_call | solution.py:71
  30.2 1.6 %shard_map.110 = bf16[2,128,512]{2,1,0:T(8,128)(2,1)S(1)} custom-call(bf16[128,4096]{1,0:T(8,128)(2,1)S(1)} %get-tuple-element.38.q_ref.refs_0_.refs_2_, bf16[128,4096]{1,0:T(8,128)(2,1)S(1)} %get-tuple-element.39.g_ref.refs_1_.refs_3_, f32[4,8,1024]{2,1,0:T(8,128)S(1)} %get-tuple-element.49.refs_2_.refs_4_.final_ref, ...), custom_call_target="tpu_custom_call" | custom-call | flops 100000000 | bytes 100000 | tf_op jit(solution)/shard_map/pallas_call | solution.py:71
  31.8 1.3 %collective-permute-start.11 = (bf16[2,128,512]{2,1,0:T(8,128)(2,1)S(1)}, bf16[2,128,512]{2,1,0:T(8,128)(2,1)S(1)}, u32[]{:S(2)}, u32[]{:S(2)}) collective-permute-start(bf16[2,128,512]{2,1,0:T(8,128)(2,1)S(1)} %shard_map.110), channel_id=1, source_target_pairs={{1,0},{2,1},{3,2},{4,3},{5,4},{6,5},{7,6},{9,8},{10,9},{11,10},{12... | collective-permute-start | bytes 786440 | tf_op jit(solution)/shard_map/ppermute | solution.py:32
  33.1 0.6 %collective-permute-start.12 = (bf16[2,16,512]{2,1,0:T(8,128)(2,1)S(1)}, bf16[2,16,512]{2,1,0:T(8,128)(2,1)S(1)}, u32[]{:S(2)}, u32[]{:S(2)}) collective-permute-start(bf16[2,16,512]{2,1,0:T(8,128)(2,1)S(1)} %get-tuple-element.59), channel_id=1, source_target_pairs={{0,8},{8,0},{16,24},{24,16},{1,9},{9,1},{17,25},{25,17},{2,10},{10... | collective-permute-start | bytes 98312 | tf_op jit(solution)/shard_map/ppermute | solution.py:38
  33.7 1.2 %collective-permute-start.13 = (bf16[2,16,512]{2,1,0:T(8,128)(2,1)S(1)}, bf16[2,16,512]{2,1,0:T(8,128)(2,1)S(1)}, u32[]{:S(2)}, u32[]{:S(2)}) collective-permute-start(bf16[2,16,512]{2,1,0:T(8,128)(2,1)S(1)} %get-tuple-element.60), channel_id=1, source_target_pairs={{0,16},{8,24},{16,0},{24,8},{1,17},{9,25},{17,1},{25,9},{2,18},{10... | collective-permute-start | bytes 98312 | tf_op jit(solution)/shard_map/ppermute | solution.py:38
  34.9 0.2 collective-permute-start.14
  35.1 0.0 collective-permute-done.12.refs_5_
  35.1 2.5 %collective-permute-done.13.refs_6_ = bf16[2,16,512]{2,1,0:T(8,128)(2,1)S(1)} collective-permute-done((bf16[2,16,512]{2,1,0:T(8,128)(2,1)S(1)}, bf16[2,16,512]{2,1,0:T(8,128)(2,1)S(1)}, u32[]{:S(2)}, u32[]{:S(2)}) %collective-permute-start.13) | collective-permute-done | bytes 32800 | tf_op jit(solution)/shard_map/ppermute | solution.py:38
  37.6 1.0 %collective-permute-done.14.refs_7_ = bf16[2,16,512]{2,1,0:T(8,128)(2,1)S(1)} collective-permute-done((bf16[2,16,512]{2,1,0:T(8,128)(2,1)S(1)}, bf16[2,16,512]{2,1,0:T(8,128)(2,1)S(1)}, u32[]{:S(2)}, u32[]{:S(2)}) %collective-permute-start.14) | collective-permute-done | bytes 32800 | tf_op jit(solution)/shard_map/ppermute | solution.py:38
  38.5 0.2 shard_map.112
  38.8 2.1 %collective-permute-start.15 = (bf16[4,2,16,512]{3,2,1,0:T(8,128)(2,1)S(1)}, bf16[4,2,16,512]{3,2,1,0:T(8,128)(2,1)S(1)}, u32[]{:S(2)}, u32[]{:S(2)}) collective-permute-start(bf16[4,2,16,512]{3,2,1,0:T(8,128)(2,1)S(1)} %get-tuple-element.63), channel_id=1, source_target_pairs={{0,1},{1,0},{2,3},{3,2},{4,5},{5,4},{6,7},{7,6},{8,9},{9,8},{10,11... | collective-permute-start | bytes 393224 | tf_op jit(solution)/shard_map/ppermute | solution.py:38
  40.9 4.3 %collective-permute-done.15.got_ref = bf16[4,2,16,512]{3,2,1,0:T(8,128)(2,1)S(1)} collective-permute-done((bf16[4,2,16,512]{3,2,1,0:T(8,128)(2,1)S(1)}, bf16[4,2,16,512]{3,2,1,0:T(8,128)(2,1)S(1)}, u32[]{:S(2)}, u32[]{:S(2)}) %collective-permute-start.15) | collective-permute-done | bytes 131104 | tf_op jit(solution)/shard_map/ppermute | solution.py:38
  45.2 2.2 %collective-permute-start.16 = (bf16[1,2,16,512]{3,2,1,0:T(8,128)(2,1)S(1)}, bf16[1,2,16,512]{3,2,1,0:T(8,128)(2,1)S(1)}, u32[]{:S(2)}, u32[]{:S(2)}) collective-permute-start(bf16[1,2,16,512]{3,2,1,0:T(8,128)(2,1)S(1)} %get-tuple-element.65), channel_id=1, source_target_pairs={{0,2},{1,3},{2,0},{3,1},{4,6},{5,7},{6,4},{7,5},{8,10},{9,11},{10,... | collective-permute-start | bytes 98312 | tf_op jit(solution)/shard_map/ppermute | solution.py:38
  47.4 3.0 %collective-permute-start.17 = (bf16[1,2,16,512]{3,2,1,0:T(8,128)(2,1)S(1)}, bf16[1,2,16,512]{3,2,1,0:T(8,128)(2,1)S(1)}, u32[]{:S(2)}, u32[]{:S(2)}) collective-permute-start(bf16[1,2,16,512]{3,2,1,0:T(8,128)(2,1)S(1)} %get-tuple-element.66), channel_id=1, source_target_pairs={{0,4},{1,5},{2,6},{3,7},{4,0},{5,1},{6,2},{7,3},{8,12},{9,13},{10,... | collective-permute-start | bytes 98312 | tf_op jit(solution)/shard_map/ppermute | solution.py:38
  50.4 0.0 collective-permute-start.18
  50.4 2.7 %shard_map.108 = (bf16[128,4096]{1,0:T(8,128)(2,1)}, bf16[128,4096]{1,0:T(8,128)(2,1)}, f32[2,128,256]{2,1,0:T(8,128)S(1)}) custom-call(bf16[128,4096]{1,0:T(8,128)(2,1)S(1)} %get-tuple-element.38.q_ref.refs_0_.refs_2_, bf16[128,4096]{1,0:T(8,128)(2,1)S(1)} %get-tuple-element.39.g_ref.refs_1_.refs_3_, ...), custom_call_target="tpu_custom_call" | custom-call | flops 100000000 | bytes 100000 | tf_op jit(solution)/shard_map/pallas_call | solution.py:71
  53.1 2.7 %shard_map.109 = (bf16[128,4096]{1,0:T(8,128)(2,1)}, bf16[128,4096]{1,0:T(8,128)(2,1)}, f32[2,128,256]{2,1,0:T(8,128)S(1)}) custom-call(bf16[128,4096]{1,0:T(8,128)(2,1)} %get-tuple-element.52.refs_0_, bf16[128,4096]{1,0:T(8,128)(2,1)} %get-tuple-element.53.refs_1_, ...), custom_call_target="tpu_custom_call", output_to_operand_aliasing={{0}: (0, {}), {1}: (1, {})} | custom-call | flops 100000000 | bytes 100000 | tf_op jit(solution)/shard_map/pallas_call | solution.py:71
  55.8 0.0 collective-permute-done.16.refs_0_
  55.8 0.0 collective-permute-done.17.refs_1_
  55.8 0.3 collective-permute-done.18.refs_2_
  56.2 0.6 %copy.17 = f32[1,1,2,16,512]{4,3,2,1,0:T(8,128)} copy(f32[1,1,2,16,512]{4,3,2,1,0:T(8,128)S(1)} %bitcast.12) | data formatting | bytes 131072
  56.8 0.0 collective-permute-done.11.next_ref
  56.8 0.2 shard_map.111
  57.0 0.8 %copy.16 = f32[1,128,2,512]{3,2,1,0:T(2,128)} copy(f32[1,128,2,512]{3,2,1,0:T(2,128)S(1)} %bitcast.11) | data formatting | bytes 1048576
  (3 shorter events, 0.1 us)
Async XLA Ops:
  1.6 5.8 %copy-start = (bf16[1,1,2,16,512]{4,3,2,1,0:T(8,128)(2,1)S(1)}, bf16[1,1,2,16,512]{4,3,2,1,0:T(8,128)(2,1)}, u32[]{:S(2)}) copy-start(bf16[1,1,2,16,512]{4,3,2,1,0:T(8,128)(2,1)} %param.10) | copy-start | bytes 98308
  2.5 24.8 %collective-permute-start = (bf16[144,1024]{1,0:T(8,128)(2,1)S(1)}, bf16[144,1024]{1,0:T(8,128)(2,1)S(1)}, u32[]{:S(2)}, u32[]{:S(2)}) collective-permute-start(bf16[144,1024]{1,0:T(8,128)(2,1)S(1)} %get-tuple-element.37.kv_ref.refs_4_.refs_6_), channel_id=1, source_target_pairs={{0,1},{1,2},{2,3},{3,4},{4,5},{5,6},{6,7},{8,9},{9,10},{10,11},{11... | collective-permute-start | bytes 884744 | tf_op jit(solution)/shard_map/ppermute | solution.py:32
  7.4 4.5 %collective-permute-start.1 = (bf16[1,2,16,512]{3,2,1,0:T(8,128)(2,1)S(1)}, bf16[1,2,16,512]{3,2,1,0:T(8,128)(2,1)S(1)}, u32[]{:S(2)}, u32[]{:S(2)}) collective-permute-start(bf16[1,2,16,512]{3,2,1,0:T(8,128)(2,1)S(1)} %bitcast.20), channel_id=1, source_target_pairs={{0,2},{1,3},{2,0},{3,1},{4,6},{5,7},{6,4},{7,5},{8,10},{9,11},{10,... | collective-permute-start | bytes 98312 | tf_op jit(solution)/shard_map/ppermute | solution.py:38
  9.1 5.1 %collective-permute-start.2 = (bf16[1,2,16,512]{3,2,1,0:T(8,128)(2,1)S(1)}, bf16[1,2,16,512]{3,2,1,0:T(8,128)(2,1)S(1)}, u32[]{:S(2)}, u32[]{:S(2)}) collective-permute-start(bf16[1,2,16,512]{3,2,1,0:T(8,128)(2,1)S(1)} %bitcast.21), channel_id=1, source_target_pairs={{0,4},{1,5},{2,6},{3,7},{4,0},{5,1},{6,2},{7,3},{8,12},{9,13},{10,... | collective-permute-start | bytes 98312 | tf_op jit(solution)/shard_map/ppermute | solution.py:38
  11.6 5.7 %collective-permute-start.3 = (bf16[1,2,16,512]{3,2,1,0:T(8,128)(2,1)S(1)}, bf16[1,2,16,512]{3,2,1,0:T(8,128)(2,1)S(1)}, u32[]{:S(2)}, u32[]{:S(2)}) collective-permute-start(bf16[1,2,16,512]{3,2,1,0:T(8,128)(2,1)S(1)} %bitcast.22), channel_id=1, source_target_pairs={{0,6},{1,7},{2,4},{3,5},{4,2},{5,3},{6,0},{7,1},{8,14},{9,15},{10,... | collective-permute-start | bytes 98312 | tf_op jit(solution)/shard_map/ppermute | solution.py:38
  17.4 0.7 %copy-start.1 = (s32[1,1,4]{2,1,0:T(1,128)S(1)}, s32[1,1,4]{2,1,0:T(1,128)}, u32[]{:S(2)}) copy-start(s32[1,1,4]{2,1,0:T(1,128)} %param.13) | copy-start | bytes 52
  17.4 5.1 %collective-permute-start.4 = (bf16[4,2,16,512]{3,2,1,0:T(8,128)(2,1)S(1)}, bf16[4,2,16,512]{3,2,1,0:T(8,128)(2,1)S(1)}, u32[]{:S(2)}, u32[]{:S(2)}) collective-permute-start(bf16[4,2,16,512]{3,2,1,0:T(8,128)(2,1)S(1)} %shard_map.105.near_ref), channel_id=1, source_target_pairs={{0,1},{1,0},{2,3},{3,2},{4,5},{5,4},{6,7},{7,6},{8,9},{9,8},{10,11... | collective-permute-start | bytes 393224 | tf_op jit(solution)/shard_map/ppermute | solution.py:38
  18.0 1.9 %collective-permute-start.5 = (s32[1,4]{1,0:T(1,128)S(1)}, s32[1,4]{1,0:T(1,128)S(1)}, u32[]{:S(2)}, u32[]{:S(2)}) collective-permute-start(s32[1,4]{1,0:T(1,128)S(1)} %bitcast.24), channel_id=1, source_target_pairs={{0,8},{8,0},{16,24},{24,16},{1,9},{9,1},{17,25},{25,17},{2,10},{10... | collective-permute-start | bytes 56 | tf_op jit(solution)/shard_map/ppermute | solution.py:38
  18.0 3.6 %collective-permute-start.6 = (s32[1,4]{1,0:T(1,128)S(1)}, s32[1,4]{1,0:T(1,128)S(1)}, u32[]{:S(2)}, u32[]{:S(2)}) collective-permute-start(s32[1,4]{1,0:T(1,128)S(1)} %bitcast.25), channel_id=1, source_target_pairs={{0,16},{8,24},{16,0},{24,8},{1,17},{9,25},{17,1},{25,9},{2,18},{10... | collective-permute-start | bytes 56 | tf_op jit(solution)/shard_map/ppermute | solution.py:38
  19.5 3.0 %collective-permute-start.7 = (s32[1,4]{1,0:T(1,128)S(1)}, s32[1,4]{1,0:T(1,128)S(1)}, u32[]{:S(2)}, u32[]{:S(2)}) collective-permute-start(s32[1,4]{1,0:T(1,128)S(1)} %bitcast.26), channel_id=1, source_target_pairs={{0,24},{8,16},{16,8},{24,0},{1,25},{9,17},{17,9},{25,1},{2,26},{10... | collective-permute-start | bytes 56 | tf_op jit(solution)/shard_map/ppermute | solution.py:38
  22.8 5.6 %collective-permute-start.8 = (bf16[2,16,512]{2,1,0:T(8,128)(2,1)S(1)}, bf16[2,16,512]{2,1,0:T(8,128)(2,1)S(1)}, u32[]{:S(2)}, u32[]{:S(2)}) collective-permute-start(bf16[2,16,512]{2,1,0:T(8,128)(2,1)S(1)} %get-tuple-element.46), channel_id=1, source_target_pairs={{0,8},{8,0},{16,24},{24,16},{1,9},{9,1},{17,25},{25,17},{2,10},{10... | collective-permute-start | bytes 98312 | tf_op jit(solution)/shard_map/ppermute | solution.py:38
  23.0 5.3 %collective-permute-start.9 = (bf16[2,16,512]{2,1,0:T(8,128)(2,1)S(1)}, bf16[2,16,512]{2,1,0:T(8,128)(2,1)S(1)}, u32[]{:S(2)}, u32[]{:S(2)}) collective-permute-start(bf16[2,16,512]{2,1,0:T(8,128)(2,1)S(1)} %get-tuple-element.47), channel_id=1, source_target_pairs={{0,16},{8,24},{16,0},{24,8},{1,17},{9,25},{17,1},{25,9},{2,18},{10... | collective-permute-start | bytes 98312 | tf_op jit(solution)/shard_map/ppermute | solution.py:38
  24.3 4.1 %collective-permute-start.10 = (bf16[2,16,512]{2,1,0:T(8,128)(2,1)S(1)}, bf16[2,16,512]{2,1,0:T(8,128)(2,1)S(1)}, u32[]{:S(2)}, u32[]{:S(2)}) collective-permute-start(bf16[2,16,512]{2,1,0:T(8,128)(2,1)S(1)} %get-tuple-element.48), channel_id=1, source_target_pairs={{0,24},{8,16},{16,8},{24,0},{1,25},{9,17},{17,9},{25,1},{2,26},{10... | collective-permute-start | bytes 98312 | tf_op jit(solution)/shard_map/ppermute | solution.py:38
  31.8 25.0 %collective-permute-start.11 = (bf16[2,128,512]{2,1,0:T(8,128)(2,1)S(1)}, bf16[2,128,512]{2,1,0:T(8,128)(2,1)S(1)}, u32[]{:S(2)}, u32[]{:S(2)}) collective-permute-start(bf16[2,128,512]{2,1,0:T(8,128)(2,1)S(1)} %shard_map.110), channel_id=1, source_target_pairs={{1,0},{2,1},{3,2},{4,3},{5,4},{6,5},{7,6},{9,8},{10,9},{11,10},{12... | collective-permute-start | bytes 786440 | tf_op jit(solution)/shard_map/ppermute | solution.py:32
  33.1 2.0 %collective-permute-start.12 = (bf16[2,16,512]{2,1,0:T(8,128)(2,1)S(1)}, bf16[2,16,512]{2,1,0:T(8,128)(2,1)S(1)}, u32[]{:S(2)}, u32[]{:S(2)}) collective-permute-start(bf16[2,16,512]{2,1,0:T(8,128)(2,1)S(1)} %get-tuple-element.59), channel_id=1, source_target_pairs={{0,8},{8,0},{16,24},{24,16},{1,9},{9,1},{17,25},{25,17},{2,10},{10... | collective-permute-start | bytes 98312 | tf_op jit(solution)/shard_map/ppermute | solution.py:38
  33.7 3.9 %collective-permute-start.13 = (bf16[2,16,512]{2,1,0:T(8,128)(2,1)S(1)}, bf16[2,16,512]{2,1,0:T(8,128)(2,1)S(1)}, u32[]{:S(2)}, u32[]{:S(2)}) collective-permute-start(bf16[2,16,512]{2,1,0:T(8,128)(2,1)S(1)} %get-tuple-element.60), channel_id=1, source_target_pairs={{0,16},{8,24},{16,0},{24,8},{1,17},{9,25},{17,1},{25,9},{2,18},{10... | collective-permute-start | bytes 98312 | tf_op jit(solution)/shard_map/ppermute | solution.py:38
  34.9 3.6 %collective-permute-start.14 = (bf16[2,16,512]{2,1,0:T(8,128)(2,1)S(1)}, bf16[2,16,512]{2,1,0:T(8,128)(2,1)S(1)}, u32[]{:S(2)}, u32[]{:S(2)}) collective-permute-start(bf16[2,16,512]{2,1,0:T(8,128)(2,1)S(1)} %get-tuple-element.61), channel_id=1, source_target_pairs={{0,24},{8,16},{16,8},{24,0},{1,25},{9,17},{17,9},{25,1},{2,26},{10... | collective-permute-start | bytes 98312 | tf_op jit(solution)/shard_map/ppermute | solution.py:38
  38.8 6.4 %collective-permute-start.15 = (bf16[4,2,16,512]{3,2,1,0:T(8,128)(2,1)S(1)}, bf16[4,2,16,512]{3,2,1,0:T(8,128)(2,1)S(1)}, u32[]{:S(2)}, u32[]{:S(2)}) collective-permute-start(bf16[4,2,16,512]{3,2,1,0:T(8,128)(2,1)S(1)} %get-tuple-element.63), channel_id=1, source_target_pairs={{0,1},{1,0},{2,3},{3,2},{4,5},{5,4},{6,7},{7,6},{8,9},{9,8},{10,11... | collective-permute-start | bytes 393224 | tf_op jit(solution)/shard_map/ppermute | solution.py:38
  45.2 10.6 %collective-permute-start.16 = (bf16[1,2,16,512]{3,2,1,0:T(8,128)(2,1)S(1)}, bf16[1,2,16,512]{3,2,1,0:T(8,128)(2,1)S(1)}, u32[]{:S(2)}, u32[]{:S(2)}) collective-permute-start(bf16[1,2,16,512]{3,2,1,0:T(8,128)(2,1)S(1)} %get-tuple-element.65), channel_id=1, source_target_pairs={{0,2},{1,3},{2,0},{3,1},{4,6},{5,7},{6,4},{7,5},{8,10},{9,11},{10,... | collective-permute-start | bytes 98312 | tf_op jit(solution)/shard_map/ppermute | solution.py:38
  47.4 8.4 %collective-permute-start.17 = (bf16[1,2,16,512]{3,2,1,0:T(8,128)(2,1)S(1)}, bf16[1,2,16,512]{3,2,1,0:T(8,128)(2,1)S(1)}, u32[]{:S(2)}, u32[]{:S(2)}) collective-permute-start(bf16[1,2,16,512]{3,2,1,0:T(8,128)(2,1)S(1)} %get-tuple-element.66), channel_id=1, source_target_pairs={{0,4},{1,5},{2,6},{3,7},{4,0},{5,1},{6,2},{7,3},{8,12},{9,13},{10,... | collective-permute-start | bytes 98312 | tf_op jit(solution)/shard_map/ppermute | solution.py:38
  50.4 5.7 %collective-permute-start.18 = (bf16[1,2,16,512]{3,2,1,0:T(8,128)(2,1)S(1)}, bf16[1,2,16,512]{3,2,1,0:T(8,128)(2,1)S(1)}, u32[]{:S(2)}, u32[]{:S(2)}) collective-permute-start(bf16[1,2,16,512]{3,2,1,0:T(8,128)(2,1)S(1)} %get-tuple-element.67), channel_id=1, source_target_pairs={{0,6},{1,7},{2,4},{3,5},{4,2},{5,3},{6,0},{7,1},{8,14},{9,15},{10,... | collective-permute-start | bytes 98312 | tf_op jit(solution)/shard_map/ppermute | solution.py:38

commit v4 on v3

--- a/solution.py
+++ b/solution.py
@@ -86,9 +86,13 @@
 
 
 def pack_kernel(
-    ids_hbm, owners_hbm, seg_hbm, kv_ref, ids_ref, owners_ref, seg_ref, payload_ref, sems
+    ids_hbm, owners_hbm, seg_hbm, reach_hbm, q_hbm, g_hbm, kv_ref,
+    ids_ref, owners_ref, seg_ref, reach_ref, q_ref, g_ref, payload_ref, sems,
 ):
-    pairs = ((ids_hbm, ids_ref), (owners_hbm, owners_ref), (seg_hbm, seg_ref))
+    pairs = (
+        (ids_hbm, ids_ref), (owners_hbm, owners_ref), (seg_hbm, seg_ref),
+        (reach_hbm, reach_ref), (q_hbm, q_ref), (g_hbm, g_ref),
+    )
     copies = [pltpu.make_async_copy(src, dst, sems.at[i]) for i, (src, dst) in enumerate(pairs)]
     for copy in copies:
         copy.start()
@@ -106,28 +110,16 @@
 
 
 def own_kernel(
-    reach_hbm, q_hbm, g_hbm, ids_ref, kv_ref,
-    q_ref, g_ref, stats_ref, bias_ref, tbias_ref, reach_ref, sems,
+    reach_ref, ids_ref, kv_ref, q_ref, g_ref, stats_ref, bias_ref, tbias_ref
 ):
     n = q_ref.shape[0]
     heads = stats_ref.shape[0]
-    part = GROUP * DH
-    first = pltpu.make_async_copy(reach_hbm, reach_ref, sems.at[2, 0])
-    first.start()
-    copies = []
-    for h in range(heads):
-        some = pl.ds(h * part, part)
-        for i, (src, dst) in enumerate(((q_hbm, q_ref), (g_hbm, g_ref))):
-            copy = pltpu.make_async_copy(src.at[:, some], dst.at[:, some], sems.at[i, h])
-            copy.start()
-            copies.append(copy)
     ids = ids_ref[...]
     id_cols = jnp.broadcast_to(ids.astype(F32), (n, n))
     k_idx = lax.broadcasted_iota(jnp.int32, (n, n), 0)
     q_idx = lax.broadcasted_iota(jnp.int32, (n, n), 1)
     bias_ref[...] = as_bias((id_cols.T == id_cols) & (k_idx <= q_idx))
     bias = tile_heads(bias_ref[...])
-    first.wait()
     reach_row = jnp.zeros((1, n), jnp.int32)
     for b in range(reach_ref.shape[1]):
         reach_row = jnp.where(ids == b, reach_ref[0:1, b : b + 1], reach_row)
@@ -138,8 +130,6 @@
         row = as_bias((me ^ k) < reach_row)
         tbias_ref[k * seg_len : (k + 1) * seg_len] = jnp.broadcast_to(row, (seg_len, n))
     for h in range(heads):
-        copies[2 * h].wait()
-        copies[2 * h + 1].wait()
         scores, grad_w = scored(
             kv_ref[:n, cols(h)], kv_ref[:n, cols(h + heads)],
             head_rows(q_ref, h), head_rows(g_ref, h), bias,
@@ -351,15 +341,16 @@
     for k in steps:
         pieces.append(swap(trunk_kv[0], "branch", k))
     own_kv = keys_values[0].reshape(n, 2 * kv_width)
-    ids, own_owners, own_seg, payload = call(
+    ids, own_owners, own_seg, reach, q, g, payload = call(
         pack_kernel,
         [
-            ((1, n), jnp.int32), ((1, depths), jnp.int32),
-            ((1,) + seg_shape, BF), ((n + PACK, 2 * kv_width), BF),
+            ((1, n), jnp.int32), ((1, depths), jnp.int32), ((1,) + seg_shape, BF),
+            (branch_reach.shape, jnp.int32), ((n, width), BF), ((n, width), BF),
+            ((n + PACK, 2 * kv_width), BF),
         ],
-        branch_of, ancestors[0], trunk_kv[0], own_kv,
-        hbm=3,
-        scratch=[pltpu.SemaphoreType.DMA((3,))],
+        branch_of, ancestors[0], trunk_kv[0], branch_reach, queries[0], out_grad[0], own_kv,
+        hbm=6,
+        scratch=[pltpu.SemaphoreType.DMA((6,))],
     )
     earlier = ring(payload, "branch", 1, CHAIN_F)
     owners = [own_owners]
@@ -367,14 +358,8 @@
         owners.append(swap(ancestors[0], "trunk", k))
     (near,) = call(join_kernel, [((n_branch // 2,) + seg_shape, BF)], own_seg, *pieces)
     far = swap(near, "branch", 1)
-    q, g, stats0, obias, tbias = call(
-        own_kernel,
-        [((n, width), BF), ((n, width), BF), stats_shape, bias_shape, tbias_shape],
-        branch_reach, queries[0], out_grad[0], ids, payload,
-        hbm=3,
-        scratch=[
-            pltpu.VMEM(branch_reach.shape, jnp.int32), pltpu.SemaphoreType.DMA((3, heads)),
-        ],
+    stats0, obias, tbias = call(
+        own_kernel, [stats_shape, bias_shape, tbias_shape], reach, ids, payload, q, g
     )
     stats1, ebias = call(earlier_kernel, [stats_shape, bias_shape], ids, q, g, earlier, stats0)
     picked = call(

time: 58.1 us -> 57.8 us (level)
  Pallas kernels: 13.9 us -> 13.3 us
    pallas_call x13, Pallas kernels: 13.9 us -> 13.3 us  [call(): pl.pallas_call(kernel, in_specs=[hspec] * hbm + [vspec] * (len(args) - hb...]
  transfers between devices with their start and end apart: 19 -> 19, of which waited for: 8 -> 10; matrix products, arithmetic and copies ran while one was open for 1% -> 1% of each run, Pallas kernels for 17% -> 14%
where the time goes in v4:
time: 57.8 us; the launch traced here: 57.5 us
  starting transfers between devices  24.4 us (42%)
  waiting for transfers between devices  16.1 us (28%)
  Pallas kernels  13.3 us (23%)
  local copies, waits for them, and re-layouts  2.97 us (5%)
  between operations  0.79 us (1%)
    ppermute x17, starting transfers between devices, swap(): lax.ppermute(block, axis, [(i, i ^ k) for i in range(lax.axis_size(axis))])  18.2 us
    ppermute x17, waiting for transfers between devices, swap(): lax.ppermute(block, axis, [(i, i ^ k) for i in range(lax.axis_size(axis))])  16.1 us
    pallas_call x13, Pallas kernels, call(): pl.pallas_call(kernel, in_specs=[hspec] * hbm + [vspec] * (len(args) - hb...  13.3 us
    ppermute x2, starting transfers between devices, ring(): return lax.ppermute(block, axis, route)  6.21 us
    unnamed x7, local copies, waits for them, and re-layouts  2.97 us
  transfers between devices with their start and end apart: 19, of which 10 were waited for; matrix products, arithmetic and copies ran while one was open for 1% of the time, Pallas kernels for 14%

profile of v4, /device:TPU:0, one launch (start us, length us, event | category | flops | bytes accessed | tf_op | source)
XLA Modules:
  0.0 57.5 jit_solution(7920143640440969332)
XLA Ops:
  0.6 1.0 %copy.13 = bf16[16,8,2,512]{3,1,2,0:T(8,128)(2,1)S(1)} copy(bf16[16,8,2,512]{3,2,1,0:T(2,128)(2,1)} %bitcast.18) | data formatting | bytes 524288
  1.6 0.0 copy-start
  1.6 1.7 %shard_map.102 = (s32[1,128]{1,0:T(1,128)S(1)}, s32[1,4]{1,0:T(1,128)S(1)}, bf16[1,2,16,512]{3,2,1,0:T(8,128)(2,1)S(1)}, s32[1,16]{1,0:T(1,128)S(1)}, bf16[128,4...) custom-call(s32[1,128]{1,0:T(1,128)} %ids_hbm.1, s32[1,4]{1,0:T(1,128)} %bitcast.23, ...), custom_call_target="tpu_custom_call" | custom-call | flops 100000000 | bytes 100000 | tf_op jit(solution)/shard_map/pallas_call | solution.py:71
  3.3 4.9 %collective-permute-start = (bf16[144,1024]{1,0:T(8,128)(2,1)S(1)}, bf16[144,1024]{1,0:T(8,128)(2,1)S(1)}, u32[]{:S(2)}, u32[]{:S(2)}) collective-permute-start(bf16[144,1024]{1,0:T(8,128)(2,1)S(1)} %get-tuple-element.40.kv_ref.refs_4_.refs_6_), channel_id=1, source_target_pairs={{0,1},{1,2},{2,3},{3,4},{4,5},{5,6},{6,7},{8,9},{9,10},{10,11},{11... | collective-permute-start | bytes 884744 | tf_op jit(solution)/shard_map/ppermute | solution.py:32
  8.2 0.0 copy-done
  8.2 1.6 %collective-permute-start.1 = (bf16[1,2,16,512]{3,2,1,0:T(8,128)(2,1)S(1)}, bf16[1,2,16,512]{3,2,1,0:T(8,128)(2,1)S(1)}, u32[]{:S(2)}, u32[]{:S(2)}) collective-permute-start(bf16[1,2,16,512]{3,2,1,0:T(8,128)(2,1)S(1)} %bitcast.20), channel_id=1, source_target_pairs={{0,2},{1,3},{2,0},{3,1},{4,6},{5,7},{6,4},{7,5},{8,10},{9,11},{10,... | collective-permute-start | bytes 98312 | tf_op jit(solution)/shard_map/ppermute | solution.py:38
  9.9 2.6 %collective-permute-start.2 = (bf16[1,2,16,512]{3,2,1,0:T(8,128)(2,1)S(1)}, bf16[1,2,16,512]{3,2,1,0:T(8,128)(2,1)S(1)}, u32[]{:S(2)}, u32[]{:S(2)}) collective-permute-start(bf16[1,2,16,512]{3,2,1,0:T(8,128)(2,1)S(1)} %bitcast.21), channel_id=1, source_target_pairs={{0,4},{1,5},{2,6},{3,7},{4,0},{5,1},{6,2},{7,3},{8,12},{9,13},{10,... | collective-permute-start | bytes 98312 | tf_op jit(solution)/shard_map/ppermute | solution.py:38
  12.5 0.2 collective-permute-start.3
  12.7 0.0 collective-permute-done.1.refs_1_
  12.7 2.3 %collective-permute-done.2.refs_2_ = bf16[1,2,16,512]{3,2,1,0:T(8,128)(2,1)S(1)} collective-permute-done((bf16[1,2,16,512]{3,2,1,0:T(8,128)(2,1)S(1)}, bf16[1,2,16,512]{3,2,1,0:T(8,128)(2,1)S(1)}, u32[]{:S(2)}, u32[]{:S(2)}) %collective-permute-start.2) | collective-permute-done | bytes 32800 | tf_op jit(solution)/shard_map/ppermute | solution.py:38
  15.0 3.2 %collective-permute-done.3.refs_3_ = bf16[1,2,16,512]{3,2,1,0:T(8,128)(2,1)S(1)} collective-permute-done((bf16[1,2,16,512]{3,2,1,0:T(8,128)(2,1)S(1)}, bf16[1,2,16,512]{3,2,1,0:T(8,128)(2,1)S(1)}, u32[]{:S(2)}, u32[]{:S(2)}) %collective-permute-start.3) | collective-permute-done | bytes 32800 | tf_op jit(solution)/shard_map/ppermute | solution.py:38
  18.2 0.0 copy-start.1
  18.2 0.1 collective-permute-start.4
  18.3 0.6 copy-done.1
  18.8 0.0 collective-permute-start.5
  18.8 1.5 %collective-permute-start.6 = (s32[1,4]{1,0:T(1,128)S(1)}, s32[1,4]{1,0:T(1,128)S(1)}, u32[]{:S(2)}, u32[]{:S(2)}) collective-permute-start(s32[1,4]{1,0:T(1,128)S(1)} %bitcast.25), channel_id=1, source_target_pairs={{0,16},{8,24},{16,0},{24,8},{1,17},{9,25},{17,1},{25,9},{2,18},{10... | collective-permute-start | bytes 56 | tf_op jit(solution)/shard_map/ppermute | solution.py:38
  20.3 0.4 collective-permute-start.7
  20.7 0.0 collective-permute-done.5.refs_1_
  20.7 1.7 %collective-permute-done.6.refs_2_ = s32[1,4]{1,0:T(1,128)S(1)} collective-permute-done((s32[1,4]{1,0:T(1,128)S(1)}, s32[1,4]{1,0:T(1,128)S(1)}, u32[]{:S(2)}, u32[]{:S(2)}) %collective-permute-start.6) | collective-permute-done | bytes 48 | tf_op jit(solution)/shard_map/ppermute | solution.py:38
  22.4 0.9 %collective-permute-done.7.refs_3_ = s32[1,4]{1,0:T(1,128)S(1)} collective-permute-done((s32[1,4]{1,0:T(1,128)S(1)}, s32[1,4]{1,0:T(1,128)S(1)}, u32[]{:S(2)}, u32[]{:S(2)}) %collective-permute-start.7) | collective-permute-done | bytes 48 | tf_op jit(solution)/shard_map/ppermute | solution.py:38
  23.3 0.0 collective-permute-done.4.far_ref
  23.3 0.2 shard_map.106
  23.6 0.3 collective-permute-start.8
  23.9 1.2 %collective-permute-start.9 = (bf16[2,16,512]{2,1,0:T(8,128)(2,1)S(1)}, bf16[2,16,512]{2,1,0:T(8,128)(2,1)S(1)}, u32[]{:S(2)}, u32[]{:S(2)}) collective-permute-start(bf16[2,16,512]{2,1,0:T(8,128)(2,1)S(1)} %get-tuple-element.49), channel_id=1, source_target_pairs={{0,16},{8,24},{16,0},{24,8},{1,17},{9,25},{17,1},{25,9},{2,18},{10... | collective-permute-start | bytes 98312 | tf_op jit(solution)/shard_map/ppermute | solution.py:38
  25.1 0.4 collective-permute-start.10
  25.5 1.1 %shard_map.103 = (f32[4,8,1024]{2,1,0:T(8,128)S(1)}, f32[128,128]{1,0:T(8,128)S(1)}, f32[64,128]{1,0:T(8,128)S(1)}) custom-call(s32[1,16]{1,0:T(1,128)S(1)} %get-tuple-element.41.reach_ref, s32[1,128]{1,0:T(1,128)S(1)} %get-tuple-element.39.ids_ref, bf16[144,1024]{1,0:T(8,128)(2,1)S(1)} %get-tuple-element.40.kv_ref.refs_4_.refs_6_, ...), custom_call_target="tpu_custom_call" | custom-call | flops 100000000 | bytes 100000 | tf_op jit(solution)/shard_map/pallas_call | solution.py:71
  26.6 0.0 collective-permute-done.kv_ref.refs_3_.refs_5_
  26.6 1.1 %shard_map.104 = (f32[4,8,1024]{2,1,0:T(8,128)S(1)}, f32[128,128]{1,0:T(8,128)S(1)}) custom-call(s32[1,128]{1,0:T(1,128)S(1)} %get-tuple-element.39.ids_ref, bf16[128,4096]{1,0:T(8,128)(2,1)S(1)} %get-tuple-element.37.q_ref.refs_0_.refs_2_, bf16[128,4096]{1,0:T(8,128)(2,1)S(1)} %get-tuple-element.38.g_ref.refs_1_.refs_3_, ...), custom_call_target="tpu_custom_call" | custom-call | flops 100000000 | bytes 100000 | tf_op jit(solution)/shard_map/pallas_call | solution.py:71
  27.7 0.0 collective-permute-done.8.refs_1_.refs_9_.refs_11_
  27.7 0.1 collective-permute-done.9.refs_2_.refs_10_.refs_12_
  27.8 0.7 %collective-permute-done.10.refs_3_.refs_11_.refs_13_ = bf16[2,16,512]{2,1,0:T(8,128)(2,1)S(1)} collective-permute-done((bf16[2,16,512]{2,1,0:T(8,128)(2,1)S(1)}, bf16[2,16,512]{2,1,0:T(8,128)(2,1)S(1)}, u32[]{:S(2)}, u32[]{:S(2)}) %collective-permute-start.10) | collective-permute-done | bytes 32800 | tf_op jit(solution)/shard_map/ppermute | solution.py:38
  28.5 1.8 %shard_map.107 = (f32[4,8,1024]{2,1,0:T(8,128)S(1)}, bf16[2,16,512]{2,1,0:T(8,128)(2,1)S(1)}, bf16[2,16,512]{2,1,0:T(8,128)(2,1)S(1)}, bf16[2,16,512]{2,1,0:T(8,128)(2,1)S(1)}, bf16[2,16,512]{2,1,0:T(8,128)(2,1)S(1)}) custom-call(bf16[128,4096]{1,0:T(8,128)(2,1)S(1)} %get-tuple-element.37.q_ref.refs_0_.refs_2_, ...), custom_call_target="tpu_custom_call" | custom-call | flops 100000000 | bytes 100000 | tf_op jit(solution)/shard_map/pallas_call | solution.py:71
  30.2 1.6 %shard_map.110 = bf16[2,128,512]{2,1,0:T(8,128)(2,1)S(1)} custom-call(bf16[128,4096]{1,0:T(8,128)(2,1)S(1)} %get-tuple-element.37.q_ref.refs_0_.refs_2_, bf16[128,4096]{1,0:T(8,128)(2,1)S(1)} %get-tuple-element.38.g_ref.refs_1_.refs_3_, f32[4,8,1024]{2,1,0:T(8,128)S(1)} %get-tuple-element.51.refs_2_.refs_4_.final_ref, ...), custom_call_target="tpu_custom_call" | custom-call | flops 100000000 | bytes 100000 | tf_op jit(solution)/shard_map/pallas_call | solution.py:71
  31.8 1.3 %collective-permute-start.11 = (bf16[2,128,512]{2,1,0:T(8,128)(2,1)S(1)}, bf16[2,128,512]{2,1,0:T(8,128)(2,1)S(1)}, u32[]{:S(2)}, u32[]{:S(2)}) collective-permute-start(bf16[2,128,512]{2,1,0:T(8,128)(2,1)S(1)} %shard_map.110), channel_id=1, source_target_pairs={{1,0},{2,1},{3,2},{4,3},{5,4},{6,5},{7,6},{9,8},{10,9},{11,10},{12... | collective-permute-start | bytes 786440 | tf_op jit(solution)/shard_map/ppermute | solution.py:32
  33.1 0.2 collective-permute-start.12
  33.4 1.1 %collective-permute-start.13 = (bf16[2,16,512]{2,1,0:T(8,128)(2,1)S(1)}, bf16[2,16,512]{2,1,0:T(8,128)(2,1)S(1)}, u32[]{:S(2)}, u32[]{:S(2)}) collective-permute-start(bf16[2,16,512]{2,1,0:T(8,128)(2,1)S(1)} %get-tuple-element.62), channel_id=1, source_target_pairs={{0,16},{8,24},{16,0},{24,8},{1,17},{9,25},{17,1},{25,9},{2,18},{10... | collective-permute-start | bytes 98312 | tf_op jit(solution)/shard_map/ppermute | solution.py:38
  34.4 0.6 %collective-permute-start.14 = (bf16[2,16,512]{2,1,0:T(8,128)(2,1)S(1)}, bf16[2,16,512]{2,1,0:T(8,128)(2,1)S(1)}, u32[]{:S(2)}, u32[]{:S(2)}) collective-permute-start(bf16[2,16,512]{2,1,0:T(8,128)(2,1)S(1)} %get-tuple-element.63), channel_id=1, source_target_pairs={{0,24},{8,16},{16,8},{24,0},{1,25},{9,17},{17,9},{25,1},{2,26},{10... | collective-permute-start | bytes 98312 | tf_op jit(solution)/shard_map/ppermute | solution.py:38
  35.1 0.0 collective-permute-done.12.refs_5_
  35.1 2.2 %collective-permute-done.13.refs_6_ = bf16[2,16,512]{2,1,0:T(8,128)(2,1)S(1)} collective-permute-done((bf16[2,16,512]{2,1,0:T(8,128)(2,1)S(1)}, bf16[2,16,512]{2,1,0:T(8,128)(2,1)S(1)}, u32[]{:S(2)}, u32[]{:S(2)}) %collective-permute-start.13) | collective-permute-done | bytes 32800 | tf_op jit(solution)/shard_map/ppermute | solution.py:38
  37.3 0.6 collective-permute-done.14.refs_7_
  37.8 0.2 shard_map.112
  38.1 2.6 %collective-permute-start.15 = (bf16[4,2,16,512]{3,2,1,0:T(8,128)(2,1)S(1)}, bf16[4,2,16,512]{3,2,1,0:T(8,128)(2,1)S(1)}, u32[]{:S(2)}, u32[]{:S(2)}) collective-permute-start(bf16[4,2,16,512]{3,2,1,0:T(8,128)(2,1)S(1)} %get-tuple-element.65), channel_id=1, source_target_pairs={{0,1},{1,0},{2,3},{3,2},{4,5},{5,4},{6,7},{7,6},{8,9},{9,8},{10,11... | collective-permute-start | bytes 393224 | tf_op jit(solution)/shard_map/ppermute | solution.py:38
  40.7 4.2 %collective-permute-done.15.got_ref = bf16[4,2,16,512]{3,2,1,0:T(8,128)(2,1)S(1)} collective-permute-done((bf16[4,2,16,512]{3,2,1,0:T(8,128)(2,1)S(1)}, bf16[4,2,16,512]{3,2,1,0:T(8,128)(2,1)S(1)}, u32[]{:S(2)}, u32[]{:S(2)}) %collective-permute-start.15) | collective-permute-done | bytes 131104 | tf_op jit(solution)/shard_map/ppermute | solution.py:38
  44.9 2.4 %collective-permute-start.16 = (bf16[1,2,16,512]{3,2,1,0:T(8,128)(2,1)S(1)}, bf16[1,2,16,512]{3,2,1,0:T(8,128)(2,1)S(1)}, u32[]{:S(2)}, u32[]{:S(2)}) collective-permute-start(bf16[1,2,16,512]{3,2,1,0:T(8,128)(2,1)S(1)} %get-tuple-element.67), channel_id=1, source_target_pairs={{0,2},{1,3},{2,0},{3,1},{4,6},{5,7},{6,4},{7,5},{8,10},{9,11},{10,... | collective-permute-start | bytes 98312 | tf_op jit(solution)/shard_map/ppermute | solution.py:38
  47.4 2.8 %collective-permute-start.17 = (bf16[1,2,16,512]{3,2,1,0:T(8,128)(2,1)S(1)}, bf16[1,2,16,512]{3,2,1,0:T(8,128)(2,1)S(1)}, u32[]{:S(2)}, u32[]{:S(2)}) collective-permute-start(bf16[1,2,16,512]{3,2,1,0:T(8,128)(2,1)S(1)} %get-tuple-element.68), channel_id=1, source_target_pairs={{0,4},{1,5},{2,6},{3,7},{4,0},{5,1},{6,2},{7,3},{8,12},{9,13},{10,... | collective-permute-start | bytes 98312 | tf_op jit(solution)/shard_map/ppermute | solution.py:38
  50.2 0.0 collective-permute-start.18
  50.2 2.7 %shard_map.108 = (bf16[128,4096]{1,0:T(8,128)(2,1)}, bf16[128,4096]{1,0:T(8,128)(2,1)}, f32[2,128,256]{2,1,0:T(8,128)S(1)}) custom-call(bf16[128,4096]{1,0:T(8,128)(2,1)S(1)} %get-tuple-element.37.q_ref.refs_0_.refs_2_, bf16[128,4096]{1,0:T(8,128)(2,1)S(1)} %get-tuple-element.38.g_ref.refs_1_.refs_3_, ...), custom_call_target="tpu_custom_call" | custom-call | flops 100000000 | bytes 100000 | tf_op jit(solution)/shard_map/pallas_call | solution.py:71
  52.9 2.7 %shard_map.109 = (bf16[128,4096]{1,0:T(8,128)(2,1)}, bf16[128,4096]{1,0:T(8,128)(2,1)}, f32[2,128,256]{2,1,0:T(8,128)S(1)}) custom-call(bf16[128,4096]{1,0:T(8,128)(2,1)} %get-tuple-element.54.refs_0_, bf16[128,4096]{1,0:T(8,128)(2,1)} %get-tuple-element.55.refs_1_, ...), custom_call_target="tpu_custom_call", output_to_operand_aliasing={{0}: (0, {}), {1}: (1, {})} | custom-call | flops 100000000 | bytes 100000 | tf_op jit(solution)/shard_map/pallas_call | solution.py:71
  55.6 0.0 collective-permute-done.16.refs_0_
  55.6 0.0 collective-permute-done.17.refs_1_
  55.6 0.3 collective-permute-done.18.refs_2_
  55.9 0.6 %copy.17 = f32[1,1,2,16,512]{4,3,2,1,0:T(8,128)} copy(f32[1,1,2,16,512]{4,3,2,1,0:T(8,128)S(1)} %bitcast.12) | data formatting | bytes 131072
  56.6 0.0 collective-permute-done.11.next_ref
  56.6 0.2 shard_map.111
  56.7 0.8 %copy.16 = f32[1,128,2,512]{3,2,1,0:T(2,128)} copy(f32[1,128,2,512]{3,2,1,0:T(2,128)S(1)} %bitcast.11) | data formatting | bytes 1048576
  (3 shorter events, 0.1 us)
Async XLA Ops:
  1.6 6.6 %copy-start = (bf16[1,1,2,16,512]{4,3,2,1,0:T(8,128)(2,1)S(1)}, bf16[1,1,2,16,512]{4,3,2,1,0:T(8,128)(2,1)}, u32[]{:S(2)}) copy-start(bf16[1,1,2,16,512]{4,3,2,1,0:T(8,128)(2,1)} %param.10) | copy-start | bytes 98308
  3.3 23.3 %collective-permute-start = (bf16[144,1024]{1,0:T(8,128)(2,1)S(1)}, bf16[144,1024]{1,0:T(8,128)(2,1)S(1)}, u32[]{:S(2)}, u32[]{:S(2)}) collective-permute-start(bf16[144,1024]{1,0:T(8,128)(2,1)S(1)} %get-tuple-element.40.kv_ref.refs_4_.refs_6_), channel_id=1, source_target_pairs={{0,1},{1,2},{2,3},{3,4},{4,5},{5,6},{6,7},{8,9},{9,10},{10,11},{11... | collective-permute-start | bytes 884744 | tf_op jit(solution)/shard_map/ppermute | solution.py:32
  8.2 4.5 %collective-permute-start.1 = (bf16[1,2,16,512]{3,2,1,0:T(8,128)(2,1)S(1)}, bf16[1,2,16,512]{3,2,1,0:T(8,128)(2,1)S(1)}, u32[]{:S(2)}, u32[]{:S(2)}) collective-permute-start(bf16[1,2,16,512]{3,2,1,0:T(8,128)(2,1)S(1)} %bitcast.20), channel_id=1, source_target_pairs={{0,2},{1,3},{2,0},{3,1},{4,6},{5,7},{6,4},{7,5},{8,10},{9,11},{10,... | collective-permute-start | bytes 98312 | tf_op jit(solution)/shard_map/ppermute | solution.py:38
  9.9 5.1 %collective-permute-start.2 = (bf16[1,2,16,512]{3,2,1,0:T(8,128)(2,1)S(1)}, bf16[1,2,16,512]{3,2,1,0:T(8,128)(2,1)S(1)}, u32[]{:S(2)}, u32[]{:S(2)}) collective-permute-start(bf16[1,2,16,512]{3,2,1,0:T(8,128)(2,1)S(1)} %bitcast.21), channel_id=1, source_target_pairs={{0,4},{1,5},{2,6},{3,7},{4,0},{5,1},{6,2},{7,3},{8,12},{9,13},{10,... | collective-permute-start | bytes 98312 | tf_op jit(solution)/shard_map/ppermute | solution.py:38
  12.5 5.7 %collective-permute-start.3 = (bf16[1,2,16,512]{3,2,1,0:T(8,128)(2,1)S(1)}, bf16[1,2,16,512]{3,2,1,0:T(8,128)(2,1)S(1)}, u32[]{:S(2)}, u32[]{:S(2)}) collective-permute-start(bf16[1,2,16,512]{3,2,1,0:T(8,128)(2,1)S(1)} %bitcast.22), channel_id=1, source_target_pairs={{0,6},{1,7},{2,4},{3,5},{4,2},{5,3},{6,0},{7,1},{8,14},{9,15},{10,... | collective-permute-start | bytes 98312 | tf_op jit(solution)/shard_map/ppermute | solution.py:38
  18.2 0.7 %copy-start.1 = (s32[1,1,4]{2,1,0:T(1,128)S(1)}, s32[1,1,4]{2,1,0:T(1,128)}, u32[]{:S(2)}) copy-start(s32[1,1,4]{2,1,0:T(1,128)} %param.13) | copy-start | bytes 52
  18.2 5.1 %collective-permute-start.4 = (bf16[4,2,16,512]{3,2,1,0:T(8,128)(2,1)S(1)}, bf16[4,2,16,512]{3,2,1,0:T(8,128)(2,1)S(1)}, u32[]{:S(2)}, u32[]{:S(2)}) collective-permute-start(bf16[4,2,16,512]{3,2,1,0:T(8,128)(2,1)S(1)} %shard_map.105.near_ref), channel_id=1, source_target_pairs={{0,1},{1,0},{2,3},{3,2},{4,5},{5,4},{6,7},{7,6},{8,9},{9,8},{10,11... | collective-permute-start | bytes 393224 | tf_op jit(solution)/shard_map/ppermute | solution.py:38
  18.8 1.9 %collective-permute-start.5 = (s32[1,4]{1,0:T(1,128)S(1)}, s32[1,4]{1,0:T(1,128)S(1)}, u32[]{:S(2)}, u32[]{:S(2)}) collective-permute-start(s32[1,4]{1,0:T(1,128)S(1)} %bitcast.24), channel_id=1, source_target_pairs={{0,8},{8,0},{16,24},{24,16},{1,9},{9,1},{17,25},{25,17},{2,10},{10... | collective-permute-start | bytes 56 | tf_op jit(solution)/shard_map/ppermute | solution.py:38
  18.8 3.6 %collective-permute-start.6 = (s32[1,4]{1,0:T(1,128)S(1)}, s32[1,4]{1,0:T(1,128)S(1)}, u32[]{:S(2)}, u32[]{:S(2)}) collective-permute-start(s32[1,4]{1,0:T(1,128)S(1)} %bitcast.25), channel_id=1, source_target_pairs={{0,16},{8,24},{16,0},{24,8},{1,17},{9,25},{17,1},{25,9},{2,18},{10... | collective-permute-start | bytes 56 | tf_op jit(solution)/shard_map/ppermute | solution.py:38
  20.3 3.0 %collective-permute-start.7 = (s32[1,4]{1,0:T(1,128)S(1)}, s32[1,4]{1,0:T(1,128)S(1)}, u32[]{:S(2)}, u32[]{:S(2)}) collective-permute-start(s32[1,4]{1,0:T(1,128)S(1)} %bitcast.26), channel_id=1, source_target_pairs={{0,24},{8,16},{16,8},{24,0},{1,25},{9,17},{17,9},{25,1},{2,26},{10... | collective-permute-start | bytes 56 | tf_op jit(solution)/shard_map/ppermute | solution.py:38
  23.6 4.1 %collective-permute-start.8 = (bf16[2,16,512]{2,1,0:T(8,128)(2,1)S(1)}, bf16[2,16,512]{2,1,0:T(8,128)(2,1)S(1)}, u32[]{:S(2)}, u32[]{:S(2)}) collective-permute-start(bf16[2,16,512]{2,1,0:T(8,128)(2,1)S(1)} %get-tuple-element.48), channel_id=1, source_target_pairs={{0,8},{8,0},{16,24},{24,16},{1,9},{9,1},{17,25},{25,17},{2,10},{10... | collective-permute-start | bytes 98312 | tf_op jit(solution)/shard_map/ppermute | solution.py:38
  23.9 3.9 %collective-permute-start.9 = (bf16[2,16,512]{2,1,0:T(8,128)(2,1)S(1)}, bf16[2,16,512]{2,1,0:T(8,128)(2,1)S(1)}, u32[]{:S(2)}, u32[]{:S(2)}) collective-permute-start(bf16[2,16,512]{2,1,0:T(8,128)(2,1)S(1)} %get-tuple-element.49), channel_id=1, source_target_pairs={{0,16},{8,24},{16,0},{24,8},{1,17},{9,25},{17,1},{25,9},{2,18},{10... | collective-permute-start | bytes 98312 | tf_op jit(solution)/shard_map/ppermute | solution.py:38
  25.1 3.4 %collective-permute-start.10 = (bf16[2,16,512]{2,1,0:T(8,128)(2,1)S(1)}, bf16[2,16,512]{2,1,0:T(8,128)(2,1)S(1)}, u32[]{:S(2)}, u32[]{:S(2)}) collective-permute-start(bf16[2,16,512]{2,1,0:T(8,128)(2,1)S(1)} %get-tuple-element.50), channel_id=1, source_target_pairs={{0,24},{8,16},{16,8},{24,0},{1,25},{9,17},{17,9},{25,1},{2,26},{10... | collective-permute-start | bytes 98312 | tf_op jit(solution)/shard_map/ppermute | solution.py:38
  31.8 24.7 %collective-permute-start.11 = (bf16[2,128,512]{2,1,0:T(8,128)(2,1)S(1)}, bf16[2,128,512]{2,1,0:T(8,128)(2,1)S(1)}, u32[]{:S(2)}, u32[]{:S(2)}) collective-permute-start(bf16[2,128,512]{2,1,0:T(8,128)(2,1)S(1)} %shard_map.110), channel_id=1, source_target_pairs={{1,0},{2,1},{3,2},{4,3},{5,4},{6,5},{7,6},{9,8},{10,9},{11,10},{12... | collective-permute-start | bytes 786440 | tf_op jit(solution)/shard_map/ppermute | solution.py:32
  33.1 1.9 %collective-permute-start.12 = (bf16[2,16,512]{2,1,0:T(8,128)(2,1)S(1)}, bf16[2,16,512]{2,1,0:T(8,128)(2,1)S(1)}, u32[]{:S(2)}, u32[]{:S(2)}) collective-permute-start(bf16[2,16,512]{2,1,0:T(8,128)(2,1)S(1)} %get-tuple-element.61), channel_id=1, source_target_pairs={{0,8},{8,0},{16,24},{24,16},{1,9},{9,1},{17,25},{25,17},{2,10},{10... | collective-permute-start | bytes 98312 | tf_op jit(solution)/shard_map/ppermute | solution.py:38
  33.4 3.9 %collective-permute-start.13 = (bf16[2,16,512]{2,1,0:T(8,128)(2,1)S(1)}, bf16[2,16,512]{2,1,0:T(8,128)(2,1)S(1)}, u32[]{:S(2)}, u32[]{:S(2)}) collective-permute-start(bf16[2,16,512]{2,1,0:T(8,128)(2,1)S(1)} %get-tuple-element.62), channel_id=1, source_target_pairs={{0,16},{8,24},{16,0},{24,8},{1,17},{9,25},{17,1},{25,9},{2,18},{10... | collective-permute-start | bytes 98312 | tf_op jit(solution)/shard_map/ppermute | solution.py:38
  34.4 3.4 %collective-permute-start.14 = (bf16[2,16,512]{2,1,0:T(8,128)(2,1)S(1)}, bf16[2,16,512]{2,1,0:T(8,128)(2,1)S(1)}, u32[]{:S(2)}, u32[]{:S(2)}) collective-permute-start(bf16[2,16,512]{2,1,0:T(8,128)(2,1)S(1)} %get-tuple-element.63), channel_id=1, source_target_pairs={{0,24},{8,16},{16,8},{24,0},{1,25},{9,17},{17,9},{25,1},{2,26},{10... | collective-permute-start | bytes 98312 | tf_op jit(solution)/shard_map/ppermute | solution.py:38
  38.1 6.8 %collective-permute-start.15 = (bf16[4,2,16,512]{3,2,1,0:T(8,128)(2,1)S(1)}, bf16[4,2,16,512]{3,2,1,0:T(8,128)(2,1)S(1)}, u32[]{:S(2)}, u32[]{:S(2)}) collective-permute-start(bf16[4,2,16,512]{3,2,1,0:T(8,128)(2,1)S(1)} %get-tuple-element.65), channel_id=1, source_target_pairs={{0,1},{1,0},{2,3},{3,2},{4,5},{5,4},{6,7},{7,6},{8,9},{9,8},{10,11... | collective-permute-start | bytes 393224 | tf_op jit(solution)/shard_map/ppermute | solution.py:38
  44.9 10.7 %collective-permute-start.16 = (bf16[1,2,16,512]{3,2,1,0:T(8,128)(2,1)S(1)}, bf16[1,2,16,512]{3,2,1,0:T(8,128)(2,1)S(1)}, u32[]{:S(2)}, u32[]{:S(2)}) collective-permute-start(bf16[1,2,16,512]{3,2,1,0:T(8,128)(2,1)S(1)} %get-tuple-element.67), channel_id=1, source_target_pairs={{0,2},{1,3},{2,0},{3,1},{4,6},{5,7},{6,4},{7,5},{8,10},{9,11},{10,... | collective-permute-start | bytes 98312 | tf_op jit(solution)/shard_map/ppermute | solution.py:38
  47.4 8.2 %collective-permute-start.17 = (bf16[1,2,16,512]{3,2,1,0:T(8,128)(2,1)S(1)}, bf16[1,2,16,512]{3,2,1,0:T(8,128)(2,1)S(1)}, u32[]{:S(2)}, u32[]{:S(2)}) collective-permute-start(bf16[1,2,16,512]{3,2,1,0:T(8,128)(2,1)S(1)} %get-tuple-element.68), channel_id=1, source_target_pairs={{0,4},{1,5},{2,6},{3,7},{4,0},{5,1},{6,2},{7,3},{8,12},{9,13},{10,... | collective-permute-start | bytes 98312 | tf_op jit(solution)/shard_map/ppermute | solution.py:38
  50.2 5.7 %collective-permute-start.18 = (bf16[1,2,16,512]{3,2,1,0:T(8,128)(2,1)S(1)}, bf16[1,2,16,512]{3,2,1,0:T(8,128)(2,1)S(1)}, u32[]{:S(2)}, u32[]{:S(2)}) collective-permute-start(bf16[1,2,16,512]{3,2,1,0:T(8,128)(2,1)S(1)} %get-tuple-element.69), channel_id=1, source_target_pairs={{0,6},{1,7},{2,4},{3,5},{4,2},{5,3},{6,0},{7,1},{8,14},{9,15},{10,... | collective-permute-start | bytes 98312 | tf_op jit(solution)/shard_map/ppermute | solution.py:38
